TPU v7x, 256 devices: a whole 4x4x8 slice. The times are simulated.
256 devices in a mesh: rows: 32 (over y, x, core), feat: 8 (over z).
Axes of the slice: x: 4, y: 4, z: 8, core: 2. Of those that a mesh axis runs over, the one named last changes fastest.
Arguments:
- features: bfloat16 [32768, 2048], P('rows', 'feat'), may hold values from -6 to 6
- grad_out: bfloat16 [32768, 2048], P('rows', 'feat'), may hold values from -6 to 6
- eigvecs: float32 [2048, 2048], P('feat', 'rows'), may hold values from -1 to 1, as said below
- eigvals: float32 [2048], replicated, may hold values from 0.1 to 1, as said below
- whiten: bfloat16 [2048, 2048], P(None, 'feat'), may hold values from -0.125 to 0.125
Outputs:
- grad_in: bfloat16 [32768, 2048], P('rows', 'feat')
Inputs may be any that keep to these rules, and one draw needn't show every extreme that they name: `eigvecs`: the columns are orthonormal. `eigvals`: any two entries differ by at least 0.45 / 2048.
All inputs are finite; a program needn't handle non-finite values.
Results may differ from a plain program's by a relative error of at most 0.0074.
Values may be sent and summed in bfloat16 or wider, within the bound.
A program may use at most 128 MiB of HBM per device.

v0:
```python
import jax
import jax.numpy as jnp
from jax import lax
from jax.sharding import PartitionSpec as P


def side_by_side(arrays, axis, dim, along):
    ends, at = ([], 0)
    for a in arrays[:-1]:
        at += a.shape[along]
        ends.append(at)
    both = jnp.concatenate(arrays, axis=along)
    return tuple(jnp.split(lax.all_gather(both, axis, axis=dim, tiled=True), ends, axis=along))


def copy_for_each(shard, axis):
    copies = jnp.broadcast_to(shard, (lax.axis_size(axis), *shard.shape))
    return lax.all_to_all(copies, axis, split_axis=0, concat_axis=0, tiled=True)


def laid_out(parts, dim):
    parts = jnp.moveaxis(parts, 0, dim)
    lengths = parts.shape
    return parts.reshape(*lengths[:dim], lengths[dim] * lengths[dim + 1], *lengths[dim + 2 :])


def collect(shard, axis, dim):
    parts = copy_for_each(shard, axis)
    return laid_out(parts, dim)


def of_everyone(shard, axis):
    everything = copy_for_each(shard, axis)
    return jnp.sum(everything.astype(jnp.float32), axis=0)


def split_up(shard, dim, peers):
    before, after = (shard.shape[:dim], shard.shape[dim + 1 :])
    return jnp.moveaxis(shard.reshape(*before, peers, -1, *after), dim, 0)


def summed_on_arrival(shard, axis, dim):
    peers = lax.axis_size(axis)
    parts = lax.all_to_all(split_up(shard, dim, peers), axis, 0, 0, tiled=True)
    return jnp.sum(parts.astype(jnp.float32), axis=0)


def divided(lam_row, lam_col, first_col):
    on_diag = (
        jnp.arange(lam_row.shape[0], dtype=jnp.int32)[:, None]
        == (first_col + jnp.arange(lam_col.shape[0], dtype=jnp.int32))[None, :]
    )
    root_row = lam_row ** (-0.5)
    root_col = lam_col ** (-0.5)
    gaps_lam = lam_row[:, None] - lam_col[None, :]
    safe_gap = jnp.where(on_diag, jnp.ones_like(gaps_lam), gaps_lam)
    off_diag = (root_row[:, None] - root_col[None, :]) / safe_gap
    diag_vals = -0.5 * lam_row[:, None] ** (-1.5) + jnp.zeros_like(gaps_lam)
    return jnp.where(on_diag, diag_vals, off_diag)


def local(features, grad_out, eigvecs, eigvals, whiten):
    highest = lax.Precision.HIGHEST
    tok_rows, own_cols = features.shape
    row_count = tok_rows * lax.axis_size("rows")
    contract_rows = (((0,), (0,)), ((), ()))
    contract_last = (((1,), (1,)), ((), ()))
    piece_x, piece_g = side_by_side((features, grad_out), "feat", 1, 0)
    left_part = lax.dot_general(
        features, piece_g, contract_rows, preferred_element_type=jnp.float32
    )
    right_part = lax.dot_general(
        grad_out, piece_x, contract_rows, preferred_element_type=jnp.float32
    )
    cross_one = left_part
    cross_two = right_part
    sum_x = jnp.sum(piece_x, axis=0, dtype=jnp.float32)
    sum_g = jnp.sum(piece_g, axis=0, dtype=jnp.float32)
    cross_one, cross_two, sum_x, sum_g = (cross_one, cross_two, sum_x, sum_g)
    cross_one, cross_two, sum_x, sum_g = lax.psum((cross_one, cross_two, sum_x, sum_g), "rows")
    both_cross = cross_one + cross_two
    col_mean = sum_x / row_count
    grad_mean = sum_g / row_count
    offset = lax.axis_index("feat") * own_cols
    mean_part = lax.dynamic_slice_in_dim(col_mean, offset, own_cols)
    grad_part = lax.dynamic_slice_in_dim(grad_mean, offset, own_cols)
    sym_gram = 0.5 * (
        both_cross
        - row_count
        * (mean_part[:, None] * grad_mean[None, :] + grad_part[:, None] * col_mean[None, :])
    )
    basis_cols = collect(eigvecs, "feat", 0)
    basis_block = collect(eigvecs, "rows", 1)
    narrow = basis_cols.shape[1]
    inner_prod = jnp.dot(sym_gram, basis_cols, precision=highest)
    partial_value = lax.dot_general(basis_block, inner_prod, contract_rows, precision=highest)
    rotated = of_everyone(partial_value.astype(jnp.bfloat16), "feat").astype(jnp.float32)
    first_col = lax.axis_index("rows") * narrow
    lam_col = lax.dynamic_slice_in_dim(eigvals, first_col, narrow)
    scaled = divided(eigvals, lam_col, first_col) * rotated
    back_rot = jnp.dot(basis_block, scaled, precision=highest)
    sens_own = summed_on_arrival(
        lax.dot_general(back_rot, basis_cols, contract_last, precision=highest).astype(
            jnp.bfloat16
        ),
        "rows",
        0,
    )
    scaled_own = (2.0 / row_count * sens_own).astype(jnp.bfloat16)
    sens_scaled = collect(scaled_own, "rows", 0)
    piece_x, piece_g = side_by_side((features, grad_out), "feat", 1, 0)
    shifted = (piece_g.astype(jnp.float32) - grad_mean).astype(jnp.bfloat16)
    centered = (piece_x.astype(jnp.float32) - col_mean).astype(jnp.bfloat16)
    running = jnp.dot(shifted, whiten, preferred_element_type=jnp.float32)
    grad_in = running + lax.dot_general(
        centered, sens_scaled, contract_last, preferred_element_type=jnp.float32
    )
    return grad_in.astype(jnp.bfloat16)


def solution(mesh):
    in_specs = (P("rows", "feat"), P("rows", "feat"), P("feat", "rows"), P(), P(None, "feat"))
    out_specs = P("rows", "feat")
    return jax.shard_map(local, mesh=mesh, in_specs=in_specs, out_specs=out_specs, check_vma=False)
```

profile of v0, /device:TPU:1, one launch (start us, length us, event | category | flops | bytes accessed | tf_op | source)
XLA Modules:
  0.0 375.5 jit_solution(18292856345036790117)
XLA Ops:
  6.5 0.0 copy-start
  6.5 0.0 copy-start.6
  6.5 0.0 all-gather.2.cloned.1.call-start
  6.5 2.4 pad_maximum_fusion
  8.9 0.0 all-gather.2.cloned.1.call-update
  8.9 0.0 copy-done.6
  9.0 27.7 %all_to_all.25 = f32[8,256,64]{1,2,0:T(8,128)} all-to-all(f32[8,256,64]{1,2,0:T(8,128)S(1)} %broadcast_in_dim.11), channel_id=1, replica_groups=mesh['rows'=32,'feat'=8] {'feat'}, dimensions={0} | all-to-all | bytes 1048576 | tf_op jit(solution)/shard_map/all_to_all | solution.py:18
  36.7 1.6 broadcast_in_dim.12
  38.3 10.4 %all-to-all-start.1 = ((f32[32,256,64]{1,2,0:T(8,128)}), f32[32,256,64]{1,2,0:T(8,128)S(1)}, u32[]{:S(2)}, u32[]{:S(2)}) async-start(f32[32,256,64]{1,2,0:T(8,128)} %broadcast_in_dim.12), calls=%async_computation.1 | async-start | bytes 4194304 | tf_op jit(solution)/shard_map/all_to_all | solution.py:18
  48.7 0.0 all-reduce.3.cloned.1.call-start
  48.8 66.8 %all-gather.2.cloned.1.call-done = bf16[2048,2048]{1,0:T(8,128)(2,1)} async-done(((bf16[2048,256]{1,0:T(8,128)(2,1)}), bf16[2048,2048]{1,0:T(8,128)(2,1)}) %all-gather.2.cloned.1.call-update) | async-done | bytes 8388624 | tf_op jit(solution)/shard_map/all_gather | solution.py:13
  115.6 0.0 copy-start.1
  115.6 0.0 copy-start.5
  115.6 3.8 %fusion.9 = f32[2048,256]{1,0:T(8,128)S(1)} fusion(bf16[1024,256]{1,0:T(8,128)(2,1)} %param.6, bf16[2048,2048]{1,0:T(8,128)(2,1)} %all-gather.2.cloned.1.call-done), kind=kOutput, calls=%fused_computation.12 | convolution fusion | flops 1073741824 | bytes 6815744 | tf_op jit(solution)/shard_map/dot_general | solution.py:72
  119.4 1.0 copy-done.1
  120.4 0.0 copy-done.5
  120.4 2.7 fusion.17
  123.2 0.0 all-reduce.3.cloned.1.call-update
  123.2 1.9 copy.13
  125.1 4.3 %convert_reduce_fusion.1 = (f32[2048]{0:T(1024)S(1)}, f32[2048]{0:T(1024)S(1)}) fusion(bf16[2048,2048]{1,0:T(8,128)(2,1)} %all-gather.2.cloned.1.call-done), kind=kLoop, calls=%fused_computation.3 | loop fusion | flops 8384512 | bytes 8404992 | tf_op jit(solution)/shard_map/reduce_sum | solution.py:78
  129.3 123.8 %all-reduce = (f32[2048]{0:T(1024)S(1)}, f32[2048]{0:T(1024)S(1)}) all-reduce(f32[2048]{0:T(1024)S(1)} %get-tuple-element.6, f32[2048]{0:T(1024)S(1)} %get-tuple-element.5), channel_id=1, replica_groups=mesh['rows'=32,'feat'=8] {'rows'}, use_global_device_ids=true, to_apply=%region_3.0 | all-reduce | flops 4096 | bytes 32768 | tf_op jit(solution)/shard_map/psum | solution.py:80
  253.2 0.1 dynamic_slice.10
  253.3 0.1 dynamic_slice.11
  253.3 0.0 all-reduce.3.cloned.1.call-done
  253.3 3.5 fusion.22
  256.9 0.0 all-to-all-done.1
  256.9 0.0 copy-start.2
  256.9 2.1 fusion.21
  259.0 1.6 broadcast_in_dim.13
  260.6 0.0 copy-done.2
  260.6 0.0 copy-start.7
  260.6 3.7 all-to-all-start.2
  264.4 0.0 copy-done.7
  264.4 0.1 broadcast_power_fusion.1
  264.5 47.3 %all-to-all-done.2 = bf16[8,2048,64]{1,2,0:T(8,128)(2,1)S(1)} async-done(((bf16[8,2048,64]{1,2,0:T(8,128)(2,1)}), bf16[8,2048,64]{1,2,0:T(8,128)(2,1)S(1)}, u32[]{:S(2)}, u32[]{:S(2)}) %all-to-all-start.2) | async-done | bytes 2097184 | tf_op jit(solution)/shard_map/all_to_all | solution.py:18
  311.8 0.0 copy-start.3
  311.8 0.3 convert_reduce_fusion.2
  312.1 0.0 copy-start.4
  312.1 1.2 copy-done.3
  313.3 1.2 fusion.42
  314.6 0.0 copy-done.4
  314.6 1.8 fusion.20
  316.4 25.3 %all_to_all.26 = bf16[32,8,2048]{2,1,0:T(8,128)(2,1)S(1)} all-to-all(bf16[32,8,2048]{2,1,0:T(8,128)(2,1)S(1)} %fusion.20), channel_id=1, replica_groups=mesh['rows'=32,'feat'=8] {'rows'}, dimensions={0} | all-to-all | bytes 2097152 | tf_op jit(solution)/shard_map/all_to_all | solution.py:44
  341.7 0.2 convert_reduce_fusion.3
  341.9 0.1 broadcast_in_dim.14
  342.0 0.0 slice-start
  342.0 20.9 %all_to_all.27 = bf16[32,8,2048]{2,1,0:T(8,128)(2,1)S(1)} all-to-all(bf16[32,8,2048]{2,1,0:T(8,128)(2,1)S(1)} %broadcast_in_dim.14), channel_id=1, replica_groups=mesh['rows'=32,'feat'=8] {'rows'}, dimensions={0} | all-to-all | bytes 2097152 | tf_op jit(solution)/shard_map/all_to_all | solution.py:18
  363.0 0.0 slice-start.1
  363.0 3.6 fusion.2
  366.6 0.0 copy-done
  366.6 0.0 slice-done
  366.6 0.0 slice-done.1
  366.6 2.1 fusion.32
  (7 shorter events, 0.1 us)
Async XLA Ops:
  6.5 360.1 %copy-start = (bf16[2048,256]{1,0:T(8,128)(2,1)S(1)}, bf16[2048,256]{1,0:T(8,128)(2,1)}, u32[]{:S(2)}) copy-start(bf16[2048,256]{1,0:T(8,128)(2,1)} %param.9) | copy-start | bytes 3145732
  6.5 2.4 copy-start.6
  6.5 109.0 %all-gather.2.cloned.1.call-start = ((), (), s32[]{:S(2)}) async-start(), calls=%async_computation.5 | async-start | bytes 9437184 | tf_op jit(solution)/shard_map/all_gather | solution.py:13
  38.3 218.6 %all-to-all-start.1 = ((f32[32,256,64]{1,2,0:T(8,128)}), f32[32,256,64]{1,2,0:T(8,128)S(1)}, u32[]{:S(2)}, u32[]{:S(2)}) async-start(f32[32,256,64]{1,2,0:T(8,128)} %broadcast_in_dim.12), calls=%async_computation.1 | async-start | bytes 4194304 | tf_op jit(solution)/shard_map/all_to_all | solution.py:18
  48.7 204.6 %all-reduce.3.cloned.1.call-start = ((), (), s32[]{:S(2)}) async-start(), calls=%async_computation.6 | async-start | bytes 4194304 | tf_op jit(solution)/shard_map/psum | solution.py:80
  115.6 4.8 %copy-start.1 = (bf16[2048,2048]{1,0:T(8,128)(2,1)S(1)}, bf16[2048,2048]{1,0:T(8,128)(2,1)}, u32[]{:S(2)}) copy-start(bf16[2048,2048]{1,0:T(8,128)(2,1)} %all-gather.2.cloned.1.call-done) | copy-start | bytes 25165828
  115.6 4.8 %copy-start.5 = (bf16[1024,256]{1,0:T(8,128)(2,1)S(1)}, bf16[1024,256]{1,0:T(8,128)(2,1)}, u32[]{:S(2)}) copy-start(bf16[1024,256]{1,0:T(8,128)(2,1)} %param.5) | copy-start | bytes 1572868
  256.9 3.7 copy-start.2
  260.6 3.8 %copy-start.7 = (f32[2048]{0:T(1024)S(1)}, f32[2048]{0:T(1024)}, u32[]{:S(2)}) copy-start(f32[2048]{0:T(1024)} %param.8) | copy-start | bytes 24580
  260.6 51.1 %all-to-all-start.2 = ((bf16[8,2048,64]{1,2,0:T(8,128)(2,1)}), bf16[8,2048,64]{1,2,0:T(8,128)(2,1)S(1)}, u32[]{:S(2)}, u32[]{:S(2)}) async-start(bf16[8,2048,64]{1,2,0:T(8,128)(2,1)} %broadcast_in_dim.13), calls=%async_computation.2 | async-start | bytes 4194304 | tf_op jit(solution)/shard_map/all_to_all | solution.py:18
  311.8 1.6 copy-start.3
  312.1 2.4 copy-start.4
  342.0 24.6 %slice-start = ((s8[8388608]{0:T(1024)(128)(4,1)}), s8[4194304]{0:T(1024)(128)(4,1)S(1)}, s32[]{:S(2)}) async-start(s8[8388608]{0:T(1024)(128)(4,1)} %bitcast.23), calls=%async_computation.7 | async-start | bytes 8388608
  363.0 3.7 slice-start.1
Sparse Core Ops, SparseCore 0:
  9.0 106.4 all-gather.1
  123.3 119.2 all-reduce.2
where the time goes:
time: 376 us
  blocking collectives  198 us (53%)
  waiting for transfers between devices  114 us (30%)
  matrix products  20.9 us (6%)
  starting transfers between devices  14.2 us (4%)
  between operations  13.6 us (4%)
  local copies, waits for them, and re-layouts  7.75 us (2%)
  other arithmetic  7.15 us (2%)
    psum x1, blocking collectives, local(): lax.psum((cross_one, cross_two, sum_x, sum_g), 'rows')  124 us
    all_gather x1, waiting for transfers between devices, side_by_side(): lax.all_gather(both, axis, axis=dim, tiled=True)  66.8 us
    all_to_all x2, blocking collectives, copy_for_each(): return lax.all_to_all(copies, axis, split_axis=0, concat_axis=0, tiled=True)  48.6 us
    all_to_all x2, waiting for transfers between devices, copy_for_each(): return lax.all_to_all(copies, axis, split_axis=0, concat_axis=0, tiled=True)  47.3 us
    all_to_all x1, blocking collectives, summed_on_arrival(): parts = lax.all_to_all(split_up(shard, dim, peers), axis, 0, 0, tiled=True)  25.3 us
    all_to_all x2, starting transfers between devices, copy_for_each(): return lax.all_to_all(copies, axis, split_axis=0, concat_axis=0, tiled=True)  14.2 us
  transfers between devices with their start and end apart: 4, of which 2 were waited for; matrix products, arithmetic and copies ran while one was open for 5% of the time, Pallas kernels for 0%

commit v1 on v0

v1 whole, which is shorter than its diff:
```python
import functools

import jax
import jax.numpy as jnp
from jax import lax
from jax.experimental import pallas as pl
from jax.experimental.pallas import tpu as pltpu
from jax.sharding import PartitionSpec as P

MESH = pl.DeviceIdType.MESH
F32 = jnp.float32
BF16 = jnp.bfloat16
VMEM_CAP = 60 * 1024 * 1024


class Dims:
    def __init__(self, rows, feat, tokens, d):
        self.nr, self.nz = rows, feat
        self.nk = rows // 2
        self.nx = {4: 2, 16: 4}[self.nk]
        self.ny = self.nk // self.nx
        self.kh = self.nk // 2
        self.d, self.dh = d, d // 2
        self.n = tokens
        self.tok = tokens // rows
        self.fb = d // feat
        self.fbh = self.fb // 2
        self.sr = self.fb // self.nk
        self.ea = d // self.nk
        self.er = d // rows


def where_am_i(s):
    r = lax.axis_index("rows")
    z = lax.axis_index("feat")
    return r, z, r // 2, lax.rem(r, 2)


def send(src, dst, ss, rs, r, z):
    copy = pltpu.make_async_remote_copy(
        src, dst, ss, rs, device_id={"rows": r, "feat": z}, device_id_type=MESH
    )
    copy.start()


def arrive(ref, sem):
    pltpu.make_async_copy(ref, ref, sem).wait()


def greet(s, r, z):
    barrier = pltpu.get_barrier_semaphore()

    def plane(t, _):
        pl.semaphore_signal(
            barrier, 1, device_id={"rows": lax.rem(r + t, s.nr), "feat": z}, device_id_type=MESH
        )
        return 0

    def line(t, _):
        pl.semaphore_signal(
            barrier, 1, device_id={"rows": r, "feat": lax.rem(z + t, s.nz)}, device_id_type=MESH
        )
        return 0

    lax.fori_loop(1, s.nr, plane, 0)
    lax.fori_loop(1, s.nz, line, 0)
    pl.semaphore_wait(barrier, s.nr - 1 + s.nz - 1)


def basis_kernel(
    s, x_ref, g_ref, v_ref, vh_ref, mean_ref, xc_ref, xct_ref,
    pad, pad_in, tile, grid, m_out, m_in, ssem, rsem, p2sem, lsem,
):
    r, z, k, c = where_am_i(s)
    y, x = k // s.nx, lax.rem(k, s.nx)
    mate = r + 1 - 2 * c
    first = c == 0
    a = jnp.where(first, x, y)
    b = jnp.where(first, y, x)

    v = v_ref[...]
    twice = jnp.concatenate([v, v], axis=1)
    lane_half = lax.broadcasted_iota(jnp.int32, twice.shape, 1) // s.er
    pad[...] = jnp.where(lane_half == c, twice, 0.0).astype(BF16)
    sum_x = jnp.sum(x_ref[...].astype(F32), axis=0, keepdims=True)
    sum_g = jnp.sum(g_ref[...].astype(F32), axis=0, keepdims=True)
    m_out[0] = jnp.concatenate([sum_x, sum_g], axis=1)
    m_in[r] = m_out[0]

    greet(s, r, z)

    send(pad, pad_in, ssem.at[0], rsem.at[0], mate, z)

    def sums(t, _):
        send(m_out.at[0], m_in.at[r], ssem.at[1], rsem.at[1], lax.rem(r + t, s.nr), z)
        return 0

    lax.fori_loop(1, s.nr, sums, 0)
    arrive(pad_in, rsem.at[0])
    tile[...] = pad[...] + pad_in[...]
    grid[b, a, z] = tile[pl.ds(pl.multiple_of(c * s.fbh, s.fbh), s.fbh), :]

    def up(t, _):
        send(grid.at[b, a, z], grid.at[b, a, z], ssem.at[2], rsem.at[2], r, lax.rem(z + t, s.nz))
        return 0

    lax.fori_loop(1, s.nz, up, 0)

    arrive(m_in.at[pl.ds(0, s.nr - 1)], rsem.at[1])
    mean = jnp.sum(m_in[...], axis=0) / s.n
    mean_ref[z] = mean

    def mean_up(t, _):
        send(mean_ref.at[z], mean_ref.at[z], ssem.at[3], rsem.at[3], r, lax.rem(z + t, s.nz))
        return 0

    lax.fori_loop(1, s.nz, mean_up, 0)
    centered = (x_ref[...].astype(F32) - mean[:, : s.fb]).astype(BF16)
    xc_ref[...] = centered
    xct_ref[...] = centered.astype(F32).T.astype(BF16)

    arrive(grid.at[0, 0, pl.ds(0, s.nz - 1)], rsem.at[2])

    def along_a(t, _):
        a2 = lax.rem(a + t, s.nx)
        y2, x2 = jnp.where(first, y, a2), jnp.where(first, a2, x)
        send(grid.at[b, a], grid.at[b, a], ssem.at[4], rsem.at[4], (y2 * s.nx + x2) * 2 + c, z)
        return 0

    lax.fori_loop(1, s.nx, along_a, 0)
    arrive(grid.at[0, pl.ds(0, s.nx - 1)], rsem.at[4])

    def along_b(t, _):
        b2 = lax.rem(b + t, s.ny)
        y2, x2 = jnp.where(first, b2, y), jnp.where(first, x, b2)
        send(grid.at[b], grid.at[b], ssem.at[5], p2sem.at[t], (y2 * s.nx + x2) * 2 + c, z)
        return 0

    lax.fori_loop(1, s.ny, along_b, 0)

    def hand_out(b2):
        def each(a2, _):
            y2, x2 = jnp.where(first, b2, a2), jnp.where(first, a2, b2)
            half = y2 // (s.ny // 2)
            kk = lax.rem(y2, s.ny // 2) * s.nx + x2
            cols = pl.ds(pl.multiple_of(kk * s.ea, s.ea), s.ea)
            dst = vh_ref.at[:, c, :, cols]

            @pl.when(half == c)
            def _():
                pltpu.make_async_copy(grid.at[b2, a2], dst, lsem).start()

            @pl.when(half != c)
            def _():
                send(grid.at[b2, a2], dst, ssem.at[6], rsem.at[6], mate, z)

            return 0

        lax.fori_loop(0, s.nx, each, 0)

    hand_out(b)

    def landed(t, _):
        b2 = lax.rem(b + s.ny - t, s.ny)
        arrive(grid.at[b2], p2sem.at[t])
        hand_out(b2)
        return 0

    lax.fori_loop(1, s.ny, landed, 0)

    arrive(mean_ref.at[pl.ds(0, s.nz - 1)], rsem.at[3])
    arrive(vh_ref.at[:, c], lsem)
    arrive(vh_ref.at[:, 1 - c], rsem.at[6])
    arrive(pad, ssem.at[0])
    arrive(m_in.at[pl.ds(0, s.nr - 1)], ssem.at[1])
    arrive(grid.at[0, 0, pl.ds(0, s.nz - 1)], ssem.at[2])
    arrive(mean_ref.at[pl.ds(0, s.nz - 1)], ssem.at[3])
    arrive(grid.at[0, pl.ds(0, s.nx - 1)], ssem.at[4])
    arrive(grid.at[pl.ds(0, s.ny - 1)], ssem.at[5])
    arrive(vh_ref.at[:, c], ssem.at[6])


def eigen_kernel(
    s, xct_ref, g_ref, vh_ref, mean_ref, kk_ref, w_ref, acc_ref, sens_ref,
    vv, cp, cp_in, part, part_in, c128, t1s, t1r, mt, sy_out, sy_in, t2p, t2d, t2s, t2g,
    sp, sp_out, sp_in, ssem, rsem, lsem,
):
    r, z, k, c = where_am_i(s)
    mate = r + 1 - 2 * c
    half = k // s.kh
    mine = half == c
    kk = lax.rem(k, s.kh)
    nzh = s.nz // 2

    load_v = pltpu.make_async_copy(vh_ref, vv, lsem)
    load_v.start()
    col_sum = jnp.sum(xct_ref[...].astype(F32), axis=1, keepdims=True)

    def gram(block):
        prod = jnp.dot(xct_ref[...], g_ref[block], preferred_element_type=F32)
        nu = mean_ref[block][:, s.fb :]
        return prod - col_sum * nu

    def cols_of(q):
        return pl.ds(pl.multiple_of(q * s.fb, s.fb), s.fb)

    def gram_theirs(q, _):
        cp[1, :, cols_of(q)] = gram((1 - c) * nzh + q)
        return 0

    lax.fori_loop(0, nzh, gram_theirs, 0)
    greet(s, r, z)
    send(cp.at[1], cp_in, ssem.at[0], rsem.at[0], mate, z)

    def gram_ours(q, _):
        cp[0, :, cols_of(q)] = gram(c * nzh + q)
        return 0

    lax.fori_loop(0, nzh, gram_ours, 0)
    arrive(cp_in, rsem.at[0])

    def slab(j, _):
        rows = pl.ds(pl.multiple_of(j * s.sr, s.sr), s.sr)
        part[j] = (cp[0, rows, :] + cp_in[rows, :]).astype(BF16)
        return 0

    lax.fori_loop(0, s.nk, slab, 0)

    def scatter(t, _):
        k2 = lax.rem(k + t, s.nk)
        send(part.at[k2], part_in.at[k], ssem.at[1], rsem.at[1], 2 * k2 + c, z)
        return 0

    lax.fori_loop(1, s.nk, scatter, 0)
    part_in[k] = part[k]

    acc_ref[...] = jnp.zeros_like(acc_ref)

    def product(q, _):
        nu = mean_ref[q][:, s.fb :]
        shifted = (g_ref[q].astype(F32) - nu).astype(BF16)
        acc_ref[...] += jnp.dot(shifted, w_ref[q], preferred_element_type=F32)
        return 0

    lax.fori_loop(0, s.nz, product, 0)

    arrive(part_in.at[pl.ds(0, s.nk - 1)], rsem.at[1])
    c128[c, z] = jnp.sum(part_in[...].astype(F32), axis=0).astype(BF16)

    def up(t, _):
        send(c128.at[c, z], c128.at[c, z], ssem.at[2], rsem.at[2], r, lax.rem(z + t, s.nz))
        return 0

    lax.fori_loop(1, s.nz, up, 0)
    load_v.wait()
    arrive(c128.at[c, pl.ds(0, s.nz - 1)], rsem.at[2])
    send(c128.at[c], c128.at[c], ssem.at[3], rsem.at[3], mate, z)

    def basis_rows(h):
        return vv[pl.ds(h * nzh, nzh)].reshape(s.dh, s.dh)

    t1 = jnp.dot(c128[c].reshape(s.ea, s.dh), basis_rows(c), preferred_element_type=F32)
    arrive(c128.at[1 - c], rsem.at[3])
    t1 += jnp.dot(c128[1 - c].reshape(s.ea, s.dh), basis_rows(1 - c), preferred_element_type=F32)
    for j in range(s.kh):
        t1s[j] = t1[:, j * s.ea : (j + 1) * s.ea].astype(BF16).reshape(s.nz, s.sr, s.ea)

    def turn(t, _):
        j = lax.rem(kk + t, s.kh)
        k2 = c * s.kh + j

        @pl.when(k2 != k)
        def _():
            send(t1s.at[j], t1r.at[:, k], ssem.at[4], rsem.at[4], 2 * k2 + c, z)

        send(t1s.at[j], t1r.at[:, k], ssem.at[5], rsem.at[4], 2 * k2 + 1 - c, z)
        return 0

    lax.fori_loop(0, s.kh, turn, 0)

    @pl.when(mine)
    def _():
        t1r[:, k] = t1s[kk]
        arrive(t1r.at[:, pl.ds(0, s.nk - 1)], rsem.at[4])
        arrive(t1s.at[pl.ds(0, s.kh - 1)], ssem.at[4])

    @pl.when(jnp.logical_not(mine))
    def _():
        arrive(t1r, rsem.at[4])
        arrive(t1s, ssem.at[4])

    arrive(t1s, ssem.at[5])

    left = t1r[...].reshape(s.d, s.ea).astype(F32).T.astype(BF16)
    mt[...] = jnp.dot(left, vv[...].reshape(s.d, s.dh), preferred_element_type=F32)
    for j in range(s.kh):
        sy_out[j] = mt[:, j * s.ea : (j + 1) * s.ea].T.astype(BF16)

    def mirror(t, _):
        j = lax.rem(kk + t, s.kh)
        k2 = c * s.kh + j

        @pl.when(k2 != k)
        def _():
            send(sy_out.at[j], sy_in.at[kk], ssem.at[6], rsem.at[6], 2 * k2 + half, z)

        return 0

    lax.fori_loop(0, s.kh, mirror, 0)

    @pl.when(mine)
    def _():
        sy_in[kk] = sy_out[kk]
        arrive(sy_in.at[pl.ds(0, s.kh - 1)], rsem.at[6])
        arrive(sy_out.at[pl.ds(0, s.kh - 1)], ssem.at[6])

    @pl.when(jnp.logical_not(mine))
    def _():
        arrive(sy_in, rsem.at[6])
        arrive(sy_out, ssem.at[6])

    total = jnp.zeros((s.ea, s.fb), F32)
    own_rows = vv.at[z]
    for j in range(s.kh):
        cols = slice(j * s.ea, (j + 1) * s.ea)
        rotated = 0.5 * (mt[:, cols] + sy_in[j].astype(F32))
        weighted = (kk_ref[:, cols] * rotated).astype(BF16)
        right = own_rows[:, :, cols].reshape(s.fb, s.ea)
        total += lax.dot_general(
            weighted, right, (((1,), (1,)), ((), ())), preferred_element_type=F32
        )
    t2p[...] = total
    send(t2p, t2d, ssem.at[7], rsem.at[7], mate, z)
    arrive(t2d, rsem.at[7])
    t2s[...] = (t2p[...] + t2d[...]).astype(BF16).reshape(t2s.shape)

    def spread(t, _):
        k2 = lax.rem(k + t, s.nk)
        send(t2s.at[c], t2g.at[kk, c], ssem.at[8], rsem.at[8], 2 * k2 + half, z)
        return 0

    lax.fori_loop(1, s.nk, spread, 0)

    @pl.when(mine)
    def _():
        t2g[kk] = t2s[...]
        arrive(t2g.at[pl.ds(0, s.kh - 1)], rsem.at[8])

    @pl.when(jnp.logical_not(mine))
    def _():
        arrive(t2g, rsem.at[8])

    right2 = t2g[...].reshape(s.dh, s.fb)

    def back(q, _):
        prod = jnp.dot(vv[q].reshape(s.fb, s.dh), right2, preferred_element_type=F32)
        prod = prod * (2.0 / s.n)
        sp[q] = prod
        sp_out[q] = prod.astype(BF16)
        send(sp_out.at[q], sp_in.at[q], ssem.at[9], rsem.at[9], mate, z)
        return 0

    lax.fori_loop(0, s.nz, back, 0)
    arrive(sp_in, rsem.at[9])

    def finish(q, _):
        sens_ref[q] = (sp[q] + sp_in[q].astype(F32)).astype(BF16)
        return 0

    lax.fori_loop(0, s.nz, finish, 0)

    arrive(cp_in, ssem.at[0])
    arrive(part.at[pl.ds(0, s.nk - 1)], ssem.at[1])
    arrive(c128.at[c, pl.ds(0, s.nz - 1)], ssem.at[2])
    arrive(c128.at[c], ssem.at[3])
    arrive(t2p, ssem.at[7])
    arrive(part.at[pl.ds(0, s.nk - 1)], ssem.at[8])
    arrive(sp_out, ssem.at[9])


def final_kernel(acc_ref, x_ref, sens_ref, out_ref, total):
    q = pl.program_id(0)

    @pl.when(q == 0)
    def _():
        total[...] = acc_ref[...]

    total[...] += jnp.dot(x_ref[0], sens_ref[0], preferred_element_type=F32)

    @pl.when(q == pl.num_programs(0) - 1)
    def _():
        out_ref[...] = total[...].astype(BF16)


def vm():
    return pl.BlockSpec(memory_space=pltpu.VMEM)


def anywhere():
    return pl.BlockSpec(memory_space=pl.ANY)


def local(features, grad_out, eigvecs, eigvals, whiten):
    tok, fb = features.shape
    s = Dims(lax.axis_size("rows"), lax.axis_size("feat"), tok * lax.axis_size("rows"), whiten.shape[0])
    sd = jax.ShapeDtypeStruct
    dma = pltpu.SemaphoreType.DMA

    grad_all = lax.all_gather(grad_out, "feat", axis=0, tiled=False)

    vh, means, centered, centered_t = pl.pallas_call(
        functools.partial(basis_kernel, s),
        name="basis",
        out_shape=(
            sd((s.nz, 2, s.fbh, s.dh), BF16),
            sd((s.nz, 1, 2 * s.fb), F32),
            sd((tok, fb), BF16),
            sd((fb, tok), BF16),
        ),
        in_specs=[vm(), vm(), vm()],
        out_specs=(anywhere(), vm(), vm(), vm()),
        scratch_shapes=[
            pltpu.VMEM((s.fb, s.ea), BF16),
            pltpu.VMEM((s.fb, s.ea), BF16),
            pltpu.VMEM((s.fb, s.ea), BF16),
            pltpu.VMEM((s.ny, s.nx, s.nz, s.fbh, s.ea), BF16),
            pltpu.VMEM((1, 1, 2 * s.fb), F32),
            pltpu.VMEM((s.nr, 1, 2 * s.fb), F32),
            dma((7,)),
            dma((7,)),
            dma((s.ny,)),
            dma,
        ],
        compiler_params=pltpu.CompilerParams(
            collective_id=0, has_side_effects=True, vmem_limit_bytes=VMEM_CAP
        ),
        cost_estimate=pl.CostEstimate(flops=40_000_000_000, bytes_accessed=16_000_000, transcendentals=0),
    )(features, grad_out, eigvecs)

    centered_all = lax.all_gather(centered, "feat", axis=0, tiled=False)

    r = lax.axis_index("rows")
    k, c = r // 2, lax.rem(r, 2)
    root = eigvals ** (-0.5)
    s_row = lax.dynamic_slice_in_dim(root, k * s.ea, s.ea)[:, None]
    s_col = lax.dynamic_slice_in_dim(root, c * s.dh, s.dh)[None, :]
    both = s_row * s_col
    weights = -(both * both) / (s_row + s_col)

    acc, sens = pl.pallas_call(
        functools.partial(eigen_kernel, s),
        name="eigen",
        out_shape=(sd((tok, fb), F32), sd((s.nz, s.fb, s.fb), BF16)),
        in_specs=[vm(), vm(), anywhere(), vm(), vm(), vm()],
        out_specs=(vm(), vm()),
        scratch_shapes=[
            pltpu.VMEM((s.nz, 2, s.fbh, s.dh), BF16),
            pltpu.VMEM((2, s.fb, s.dh), F32),
            pltpu.VMEM((s.fb, s.dh), F32),
            pltpu.VMEM((s.nk, s.sr, s.dh), BF16),
            pltpu.VMEM((s.nk, s.sr, s.dh), BF16),
            pltpu.VMEM((2, s.nz, s.sr, s.dh), BF16),
            pltpu.VMEM((s.kh, s.nz, s.sr, s.ea), BF16),
            pltpu.VMEM((s.nz, s.nk, s.sr, s.ea), BF16),
            pltpu.VMEM((s.ea, s.dh), F32),
            pltpu.VMEM((s.kh, s.ea, s.ea), BF16),
            pltpu.VMEM((s.kh, s.ea, s.ea), BF16),
            pltpu.VMEM((s.ea, s.fb), F32),
            pltpu.VMEM((s.ea, s.fb), F32),
            pltpu.VMEM((2, s.ea // 2, s.fb), BF16),
            pltpu.VMEM((s.kh, 2, s.ea // 2, s.fb), BF16),
            pltpu.VMEM((s.nz, s.fb, s.fb), F32),
            pltpu.VMEM((s.nz, s.fb, s.fb), BF16),
            pltpu.VMEM((s.nz, s.fb, s.fb), BF16),
            dma((10,)),
            dma((10,)),
            dma,
        ],
        compiler_params=pltpu.CompilerParams(
            collective_id=1, has_side_effects=True, vmem_limit_bytes=VMEM_CAP
        ),
        cost_estimate=pl.CostEstimate(flops=40_000_000_000, bytes_accessed=16_000_000, transcendentals=0),
    )(centered_t, grad_all, vh, means, weights, whiten.reshape(s.nz, s.fb, fb))

    return pl.pallas_call(
        final_kernel,
        name="final",
        grid=(s.nz,),
        out_shape=sd((tok, fb), BF16),
        in_specs=[
            pl.BlockSpec((tok, fb), lambda q: (0, 0)),
            pl.BlockSpec((1, tok, fb), lambda q: (q, 0, 0)),
            pl.BlockSpec((1, fb, fb), lambda q: (q, 0, 0)),
        ],
        out_specs=pl.BlockSpec((tok, fb), lambda q: (0, 0)),
        scratch_shapes=[pltpu.VMEM((tok, fb), F32)],
        compiler_params=pltpu.CompilerParams(dimension_semantics=("arbitrary",)),
        cost_estimate=pl.CostEstimate(flops=2 * tok * s.d * fb, bytes_accessed=6_000_000, transcendentals=0),
    )(acc, centered_all, sens)


def solution(mesh):
    in_specs = (P("rows", "feat"), P("rows", "feat"), P("feat", "rows"), P(), P(None, "feat"))
    out_specs = P("rows", "feat")
    return jax.shard_map(local, mesh=mesh, in_specs=in_specs, out_specs=out_specs, check_vma=False)
```

time: 376 us -> 159 us (0.42)
  blocking collectives: 198 us -> 0 us
  Pallas kernels: 0 us -> 141 us
  waiting for transfers between devices: 114 us -> 1.26 us
  matrix products: 20.9 us -> 0 us
  starting transfers between devices: 14.2 us -> 0.04 us
  other arithmetic: 7.15 us -> 0.97 us
  local copies, waits for them, and re-layouts: 7.75 us -> 1.69 us
    pallas_call x0 -> x3, Pallas kernels: none -> 141 us  [the longest x1 73.6 us: local(): pl.pallas_call(functools.partial(eigen_kernel, s), name='eigen', out_shap...]
    psum x1 -> x0, blocking collectives: 124 us -> none  [local(): lax.psum((cross_one, cross_two, sum_x, sum_g), 'rows')]
    all_to_all x3 -> x0, blocking collectives: 73.9 us -> none  [the longest x2 48.6 us: copy_for_each(): return lax.all_to_all(copies, axis, split_axis=0, concat_axis=0, tiled=True)]
    all_gather x1 -> x2, waiting for transfers between devices: 66.8 us -> 0.53 us  [the longest x1 0.51 us: local(): grad_all = lax.all_gather(grad_out, 'feat', axis=0, tiled=False)]
    all_to_all x2 -> x0, waiting for transfers between devices: 47.3 us -> none  [copy_for_each(): return lax.all_to_all(copies, axis, split_axis=0, concat_axis=0, tiled=True)]
    dot_general x8 -> x0, matrix products: 20.9 us -> none  [the longest x1 3.79 us: local(): lax.dot_general(grad_out, piece_x, contract_rows, preferred_element_type=...]
    all_to_all x2 -> x0, starting transfers between devices: 14.2 us -> none  [copy_for_each(): return lax.all_to_all(copies, axis, split_axis=0, concat_axis=0, tiled=True)]
    reduce_sum x3 -> x0, other arithmetic: 4.77 us -> none  [the longest x1 4.27 us: local(): sum_g = jnp.sum(piece_g, axis=0, dtype=jnp.float32)]
  transfers between devices with their start and end apart: 4 -> 2, of which waited for: 2 -> 1; matrix products, arithmetic and copies ran while one was open for 5% -> 2% of each run, Pallas kernels for 0% -> 84%
where the time goes in v1:
time: 159 us
  Pallas kernels  141 us (89%)
  between operations  13.5 us (8%)
  local copies, waits for them, and re-layouts  1.69 us (1%)
    pallas_call x1, Pallas kernels, local(): pl.pallas_call(functools.partial(eigen_kernel, s), name='eigen', out_shap...  73.6 us
    pallas_call x1, Pallas kernels, local(): pl.pallas_call(functools.partial(basis_kernel, s), name='basis', out_shap...  60.5 us
    pallas_call x1, Pallas kernels, local(): pl.pallas_call(final_kernel, name='final', grid=(s.nz,), out_shape=sd((to...  7.24 us
  transfers between devices with their start and end apart: 2, of which 1 were waited for; matrix products, arithmetic and copies ran while one was open for 2% of the time, Pallas kernels for 84%

profile of v1, /device:TPU:1, one launch (start us, length us, event | category | flops | bytes accessed | tf_op | source)
XLA Modules:
  0.0 158.8 jit_solution(4261989690349798121)
XLA Ops:
  6.5 0.0 all-gather.5.cloned.1.call-start
  6.5 0.7 all-gather.5.cloned.1.call-update
  7.3 0.0 all-gather.7.cloned.1.call-start
  7.3 1.6 %copy.6.v_ref = f32[256,64]{1,0:T(8,128)} copy(f32[256,64]{0,1:T(8,128)} %param.7) | data formatting | bytes 131072 | tf_op args[2]
  8.9 0.0 copy-start
  8.9 60.5 %basis.1 = (bf16[8,2,128,1024]{3,2,1,0:T(8,128)(2,1)}, f32[8,1,512]{2,1,0:T(1,128)}, bf16[1024,256]{1,0:T(8,128)(2,1)}, bf16[256,1024]{1,0:T(8,128)(2,1)}) custom-call(bf16[1024,256]{1,0:T(8,128)(2,1)} %x_ref.1, bf16[1024,256]{1,0:T(8,128)(2,1)} %g_ref.1, f32[256,64]{1,0:T(8,128)} %copy.6.v_ref), custom_call_target="tpu_custom_call" | custom-call | flops 40000000000 | bytes 16000000 | tf_op jit(solution)/shard_map/basis/pallas_call | solution.py:411
  69.4 0.0 all-gather.7.cloned.1.call-update
  69.4 0.0 copy-done
  69.5 0.1 dynamic_slice.6
  69.5 1.0 add_divide_fusion.kk_ref
  70.5 0.5 all-gather.5.cloned.1.call-done
  71.0 73.6 %eigen.1 = (f32[1024,256]{1,0:T(8,128)}, bf16[8,256,256]{2,1,0:T(8,128)(2,1)}) custom-call(bf16[256,1024]{1,0:T(8,128)(2,1)} %get-tuple-element.11.xct_ref, bf16[8,1024,256]{2,1,0:T(8,128)(2,1)} %bitcast.4, bf16[8,2,128,1024]{3,2,1,0:T(8,128)(2,1)} %get-tuple-element.12.vh_ref, f32[8,1,512]{2,1,0:T(1,128)} %get-tuple-element.13.mean_ref, ...), custom_call_target="tpu_custom_call" | custom-call | flops 40000000000 | bytes 16000000 | tf_op jit(solution)/shard_map/eigen/pallas_call | solution.py:450
  144.7 0.0 all-gather.7.cloned.1.call-done
  144.7 7.2 %final.1 = bf16[1024,256]{1,0:T(8,128)(2,1)} custom-call(f32[1024,256]{1,0:T(8,128)} %get-tuple-element.14.acc_ref, bf16[8,1024,256]{2,1,0:T(8,128)(2,1)} %bitcast.3, bf16[8,256,256]{2,1,0:T(8,128)(2,1)} %get-tuple-element.16.sens_ref), custom_call_target="tpu_custom_call" | custom-call | flops 1073741824 | bytes 6000000 | tf_op jit(solution)/shard_map/final/pallas_call | solution.py:485
  (2 shorter events, 0.0 us)
Async XLA Ops:
  6.5 64.5 %all-gather.5.cloned.1.call-start = ((), (), s32[]{:S(2)}) async-start(), calls=%async_computation | async-start | bytes 4718592 | tf_op jit(solution)/shard_map/all_gather | solution.py:409
  7.3 137.4 %all-gather.7.cloned.1.call-start = ((), (), s32[]{:S(2)}) async-start(), calls=%async_computation.1 | async-start | bytes 4718592 | tf_op jit(solution)/shard_map/all_gather | solution.py:440
  8.9 60.5 %copy-start = (f32[2048]{0:T(1024)S(1)}, f32[2048]{0:T(1024)}, u32[]{:S(2)}) copy-start(f32[2048]{0:T(1024)} %param.8) | copy-start | bytes 24580
Sparse Core Ops, SparseCore 0:
  9.1 61.8 all-gather.4
  72.8 64.1 all-gather.6

commit v2 on v1

v2 whole, which is shorter than its diff:
```python
import functools

import jax
import jax.numpy as jnp
from jax import lax
from jax.experimental import pallas as pl
from jax.experimental.pallas import tpu as pltpu
from jax.sharding import PartitionSpec as P

MESH = pl.DeviceIdType.MESH
F32 = jnp.float32
BF16 = jnp.bfloat16
VMEM_CAP = 62 * 1024 * 1024
CHUNKS = 4


class Dims:
    def __init__(self, rows, feat, tokens, d):
        self.nr, self.nz = rows, feat
        self.nk = rows // 2
        self.nx = {4: 2, 16: 4}[self.nk]
        self.ny = self.nk // self.nx
        self.kh = self.nk // 2
        self.d, self.dh = d, d // 2
        self.n = tokens
        self.tok = tokens // rows
        self.fb = d // feat
        self.fbh = self.fb // 2
        self.sr = self.fb // self.nk
        self.ea = d // self.nk
        self.er = d // rows
        self.hops = feat // 2
        self.chunk = self.tok // CHUNKS

    def slot(self, src, g):
        dist = (g - src) % self.nz
        if dist == 0:
            return 0
        if dist == self.hops:
            return self.nz - 1
        return 2 * dist if dist < self.hops else 2 * (self.nz - dist) - 1


def where_am_i():
    r = lax.axis_index("rows")
    z = lax.axis_index("feat")
    return r, z, r // 2, lax.rem(r, 2)


def send(src, dst, ss, rs, r, z):
    copy = pltpu.make_async_remote_copy(
        src, dst, ss, rs, device_id={"rows": r, "feat": z}, device_id_type=MESH
    )
    copy.start()


def arrive(ref, sem):
    pltpu.make_async_copy(ref, ref, sem).wait()


def greet(s, r, z):
    barrier = pltpu.get_barrier_semaphore()

    def plane(t, _):
        pl.semaphore_signal(
            barrier, 1, device_id={"rows": lax.rem(r + t, s.nr), "feat": z}, device_id_type=MESH
        )
        return 0

    def line(t, _):
        pl.semaphore_signal(
            barrier, 1, device_id={"rows": r, "feat": lax.rem(z + t, s.nz)}, device_id_type=MESH
        )
        return 0

    lax.fori_loop(1, s.nr, plane, 0)
    lax.fori_loop(1, s.nz, line, 0)
    pl.semaphore_wait(barrier, s.nr - 1 + s.nz - 1)


class Ring:
    def __init__(self, s, r, z, own, buf, ssem, hsem, rsem):
        self.s, self.r, self.z = s, r, z
        self.own, self.buf = own, buf
        self.ssem, self.hsem, self.rsem = ssem, hsem, rsem

    def block(self, way, h):
        nz = self.s.nz
        return lax.rem(self.z + (nz - h if way == 0 else h), nz)

    def rows(self, q):
        return pl.ds(q * self.s.chunk, self.s.chunk)

    def start(self, way, h, q):
        s = self.s
        to = lax.rem(self.z + (1 if way == 0 else s.nz - 1), s.nz)
        blk = self.block(way, h - 1)
        src = self.own.at[self.rows(q)] if h == 1 else self.buf.at[blk, self.rows(q)]
        ss = self.hsem if h == s.hops else self.ssem
        send(src, self.buf.at[blk, self.rows(q)], ss.at[way], self.rsem.at[way, h - 1, q], self.r, to)

    def has(self, way, h, q):
        return h < self.s.hops or (q < CHUNKS // 2) == (way == 0)

    def begin(self, qs):
        for q in qs:
            for way in (0, 1):
                self.start(way, 1, q)

    def step(self, h, qs):
        for q in qs:
            for way in (0, 1):
                if self.has(way, h, q):
                    arrive(self.buf.at[0, self.rows(q)], self.rsem.at[way, h - 1, q])
                    if h < self.s.hops and self.has(way, h + 1, q):
                        self.start(way, h + 1, q)

    def drain(self):
        s = self.s
        for way in (0, 1):
            arrive(self.buf.at[pl.ds(0, s.hops - 1)], self.ssem.at[way])
            arrive(self.buf.at[0, pl.ds(0, s.tok // 2)], self.hsem.at[way])


def whole_kernel(
    s, x_ref, g_ref, v_ref, e_ref, w_ref, out_ref,
    ga, xa, grid, vv, pad, pad_in, tile, m_out, m_in, mean, xct, acc, kk_buf,
    cp, cp_in, part, part_in, c128, t1s, t1r, mt, sy_out, sy_in, t2p, t2d, t2s, t2g,
    sp, sp_out, sp_in, sens,
    ssem, rsem, p2sem, lsem, gs, gh, gr, xs, xh, xr, ds_, dr_, rs_, rr_, zr_,
):
    r, z, k, c = where_am_i()
    y, x = k // s.nx, lax.rem(k, s.nx)
    mate = r + 1 - 2 * c
    first = c == 0
    a = jnp.where(first, x, y)
    b = jnp.where(first, y, x)
    half = k // s.kh
    mine = half == c
    kk = lax.rem(k, s.kh)
    every = range(CHUNKS)
    g_ring = Ring(s, r, z, g_ref, ga, gs, gh, gr)
    x_ring = Ring(s, r, z, xa.at[z], xa, xs, xh, xr)

    v = v_ref[...]
    twice = jnp.concatenate([v, v], axis=1)
    lane_half = lax.broadcasted_iota(jnp.int32, twice.shape, 1) // s.er
    pad[...] = jnp.where(lane_half == c, twice, 0.0).astype(BF16)
    sum_x = jnp.sum(x_ref[...].astype(F32), axis=0, keepdims=True)
    sum_g = jnp.sum(g_ref[...].astype(F32), axis=0, keepdims=True)
    m_out[0] = jnp.concatenate([sum_x, sum_g], axis=1)
    m_in[r] = m_out[0]

    greet(s, r, z)

    send(pad, pad_in, ssem.at[0], rsem.at[0], mate, z)
    g_ring.begin([0])

    def sums(t, _):
        send(m_out.at[0], m_in.at[r], ssem.at[1], rsem.at[1], lax.rem(r + t, s.nr), z)
        return 0

    lax.fori_loop(1, s.nr, sums, 0)
    arrive(pad_in, rsem.at[0])
    tile[...] = pad[...] + pad_in[...]
    grid[b, a, z] = tile[pl.ds(pl.multiple_of(c * s.fbh, s.fbh), s.fbh), :]

    def up(t, _):
        send(grid.at[b, a, z], grid.at[b, a, z], ssem.at[2], rsem.at[2], r, lax.rem(z + t, s.nz))
        return 0

    lax.fori_loop(1, s.nz, up, 0)
    g_ring.begin(every[1:])
    ga[z] = g_ref[...]

    arrive(m_in.at[pl.ds(0, s.nr - 1)], rsem.at[1])
    own_mean = jnp.sum(m_in[...], axis=0) / s.n
    mean[z] = own_mean

    def mean_up(t, _):
        send(mean.at[z], mean.at[z], ssem.at[3], rsem.at[3], r, lax.rem(z + t, s.nz))
        return 0

    lax.fori_loop(1, s.nz, mean_up, 0)
    centered = (x_ref[...].astype(F32) - own_mean[:, : s.fb]).astype(BF16)
    xa[z] = centered
    xct[...] = centered.astype(F32).T.astype(BF16)
    col_sum = jnp.sum(xct[...].astype(F32), axis=1, keepdims=True)
    acc[...] = jnp.zeros_like(acc)

    def gram(slot, blk):
        nu = mean[blk][:, s.fb :]
        prod = jnp.dot(xct[...], ga[blk], preferred_element_type=F32) - col_sum * nu
        cp[slot, 0] = prod[:, : s.fbh]
        cp[slot, 1] = prod[:, s.fbh :]

    def product(blk):
        nu = mean[blk][:, s.fb :]
        shifted = (ga[blk].astype(F32) - nu).astype(BF16)
        acc[...] += jnp.dot(shifted, w_ref[blk], preferred_element_type=F32)

    def round_of(h):
        if h == 0:
            return [(0, z)]
        if h == s.hops:
            return [(s.nz - 1, g_ring.block(0, h))]
        return [(2 * h - 1, g_ring.block(0, h)), (2 * h, g_ring.block(1, h))]

    def round_start(h):
        pairs = round_of(h)
        slots = pl.ds(pairs[0][0], len(pairs))
        for slot, blk in pairs:
            gram(slot, blk)
        send(cp.at[slots, 1 - c], cp_in.at[slots], ds_.at[h], dr_.at[h], mate, z)

    def round_scatter(h):
        pairs = round_of(h)
        slots = pl.ds(pairs[0][0], len(pairs))
        arrive(cp_in.at[slots], dr_.at[h])
        for slot, _ in pairs:
            both = cp[slot, c] + cp_in[slot]
            part[:, slot] = both.reshape(s.nk, s.sr, s.fbh).astype(BF16)

        def scatter(t, _):
            k2 = lax.rem(k + t, s.nk)
            send(part.at[k2, slots], part_in.at[k, slots], rs_.at[h], rr_.at[h], 2 * k2 + c, z)
            return 0

        lax.fori_loop(1, s.nk, scatter, 0)
        part_in[k, slots] = part[k, slots]

    def round_sum(hs, batch):
        for h in hs:
            arrive(part_in.at[pl.ds(0, s.nk - 1), pl.ds(0, len(round_of(h)))], rr_.at[h])
        lo = round_of(hs[0])[0][0]
        n = round_of(hs[-1])[-1][0] + 1 - lo
        slots = pl.ds(lo, n)
        c128[c, z, slots] = jnp.sum(part_in[:, slots].astype(F32), axis=0).astype(BF16)

        def lift(t, _):
            send(
                c128.at[c, z, slots], c128.at[c, z, slots], ssem.at[9 + batch], zr_.at[batch],
                r, lax.rem(z + t, s.nz),
            )
            return 0

        lax.fori_loop(1, s.nz, lift, 0)
        return slots

    arrive(mean.at[pl.ds(0, s.nz - 1)], rsem.at[3])
    round_start(0)

    arrive(grid.at[0, 0, pl.ds(0, s.nz - 1)], rsem.at[2])

    def along_a(t, _):
        a2 = lax.rem(a + t, s.nx)
        y2, x2 = jnp.where(first, y, a2), jnp.where(first, a2, x)
        send(grid.at[b, a], grid.at[b, a], ssem.at[4], rsem.at[4], (y2 * s.nx + x2) * 2 + c, z)
        return 0

    lax.fori_loop(1, s.nx, along_a, 0)
    round_scatter(0)
    product(z)

    def along_b(t, _):
        b2 = lax.rem(b + t, s.ny)
        y2, x2 = jnp.where(first, b2, y), jnp.where(first, x, b2)
        send(grid.at[b], grid.at[b], ssem.at[5], p2sem.at[t], (y2 * s.nx + x2) * 2 + c, z)
        return 0

    def hand_out(b2):
        def each(a2, _):
            y2, x2 = jnp.where(first, b2, a2), jnp.where(first, a2, b2)
            to = y2 // (s.ny // 2)
            pos = lax.rem(y2, s.ny // 2) * s.nx + x2
            cols = pl.ds(pl.multiple_of(pos * s.ea, s.ea), s.ea)
            dst = vv.at[:, c, :, cols]

            @pl.when(to == c)
            def _():
                pltpu.make_async_copy(grid.at[b2, a2], dst, lsem).start()

            @pl.when(to != c)
            def _():
                send(grid.at[b2, a2], dst, ssem.at[6], rsem.at[6], mate, z)

            return 0

        lax.fori_loop(0, s.nx, each, 0)

    arrive(grid.at[0, pl.ds(0, s.nx - 1)], rsem.at[4])
    lax.fori_loop(1, s.ny, along_b, 0)
    g_ring.step(1, every)
    hand_out(b)

    s_row = jnp.broadcast_to(lax.rsqrt(e_ref[k]), (s.ea, s.ea)).T
    for j in range(s.kh):
        s_col = lax.rsqrt(e_ref[c * s.kh + j])
        both = s_row * s_col
        kk_buf[:, j * s.ea : (j + 1) * s.ea] = -(both * both) / (s_row + s_col)

    for h in range(1, s.hops):
        round_start(h)
        round_scatter(h)
        for _, blk in round_of(h):
            product(blk)
        if h == s.hops - 1:
            round_sum(range(0, h), 0)
        g_ring.step(h + 1, every)

    round_start(s.hops)
    x_ring.begin(every[: CHUNKS // 2])
    round_scatter(s.hops)
    product(round_of(s.hops)[0][1])

    def landed(t, _):
        b2 = lax.rem(b + s.ny - t, s.ny)
        arrive(grid.at[b2], p2sem.at[t])
        hand_out(b2)
        return 0

    lax.fori_loop(1, s.ny, landed, 0)
    round_sum([s.hops - 1], 1)
    round_sum([s.hops], 2)
    x_ring.begin(every[CHUNKS // 2 :])

    early = round_of(s.hops - 2)[-1][0] + 1
    arrive(c128.at[c, pl.ds(0, s.nz - 1), pl.ds(0, early)], zr_.at[0])
    arrive(c128.at[c, pl.ds(0, s.nz - 1), pl.ds(0, s.nz - 1 - early)], zr_.at[1])
    arrive(c128.at[c, pl.ds(0, s.nz - 1), pl.ds(0, 1)], zr_.at[2])
    send(c128.at[c], c128.at[c], ssem.at[12], rsem.at[7], mate, z)
    arrive(vv.at[:, c], lsem)
    arrive(vv.at[:, 1 - c], rsem.at[6])

    def cross_rows(h):
        bands = []
        for src in range(s.nz):
            bands.append(jnp.concatenate([c128[h, src, s.slot(src, g)] for g in range(s.nz)], axis=1))
        return jnp.concatenate(bands, axis=0)

    def basis_rows(h):
        return vv[:, h].reshape(s.dh, s.dh)

    t1 = jnp.dot(cross_rows(c), basis_rows(c), preferred_element_type=F32)
    arrive(c128.at[1 - c], rsem.at[7])
    t1 += jnp.dot(cross_rows(1 - c), basis_rows(1 - c), preferred_element_type=F32)
    for j in range(s.kh):
        t1s[j] = t1[:, j * s.ea : (j + 1) * s.ea].astype(BF16).reshape(s.nz, s.sr, s.ea)

    def turn(t, _):
        j = lax.rem(kk + t, s.kh)
        k2 = c * s.kh + j

        @pl.when(k2 != k)
        def _():
            send(t1s.at[j], t1r.at[:, k], ssem.at[7], rsem.at[8], 2 * k2 + c, z)

        send(t1s.at[j], t1r.at[:, k], ssem.at[8], rsem.at[8], 2 * k2 + 1 - c, z)
        return 0

    lax.fori_loop(0, s.kh, turn, 0)
    x_ring.step(1, every)

    @pl.when(mine)
    def _():
        t1r[:, k] = t1s[kk]
        arrive(t1r.at[:, pl.ds(0, s.nk - 1)], rsem.at[8])
        arrive(t1s.at[pl.ds(0, s.kh - 1)], ssem.at[7])

    @pl.when(jnp.logical_not(mine))
    def _():
        arrive(t1r, rsem.at[8])
        arrive(t1s, ssem.at[7])

    left = t1r[...].reshape(s.d, s.ea).astype(F32).T.astype(BF16)
    mt[...] = jnp.dot(left, vv[...].reshape(s.d, s.dh), preferred_element_type=F32)
    for j in range(s.kh):
        sy_out[j] = mt[:, j * s.ea : (j + 1) * s.ea].T.astype(BF16)

    def mirror(t, _):
        j = lax.rem(kk + t, s.kh)
        k2 = c * s.kh + j

        @pl.when(k2 != k)
        def _():
            send(sy_out.at[j], sy_in.at[kk], ssem.at[13], rsem.at[9], 2 * k2 + half, z)

        return 0

    lax.fori_loop(0, s.kh, mirror, 0)
    x_ring.step(2, every[: CHUNKS // 2])

    @pl.when(mine)
    def _():
        sy_in[kk] = sy_out[kk]
        arrive(sy_in.at[pl.ds(0, s.kh - 1)], rsem.at[9])
        arrive(sy_out.at[pl.ds(0, s.kh - 1)], ssem.at[13])

    @pl.when(jnp.logical_not(mine))
    def _():
        arrive(sy_in, rsem.at[9])
        arrive(sy_out, ssem.at[13])

    total = jnp.zeros((s.ea, s.fb), F32)
    own_rows = vv.at[z]
    for j in range(s.kh):
        cols = slice(j * s.ea, (j + 1) * s.ea)
        rotated = 0.5 * (mt[:, cols] + sy_in[j].astype(F32))
        weighted = (kk_buf[:, cols] * rotated).astype(BF16)
        right = own_rows[:, :, cols].reshape(s.fb, s.ea)
        total += lax.dot_general(
            weighted, right, (((1,), (1,)), ((), ())), preferred_element_type=F32
        )
    t2p[...] = total
    send(t2p, t2d, ssem.at[14], rsem.at[10], mate, z)
    x_ring.step(2, every[CHUNKS // 2 :])
    arrive(t2d, rsem.at[10])
    t2s[...] = (t2p[...] + t2d[...]).astype(BF16).reshape(t2s.shape)

    def spread(t, _):
        k2 = lax.rem(k + t, s.nk)
        send(t2s.at[c], t2g.at[kk, c], ssem.at[15], rsem.at[11], 2 * k2 + half, z)
        return 0

    lax.fori_loop(1, s.nk, spread, 0)
    x_ring.step(3, every)

    @pl.when(mine)
    def _():
        t2g[kk] = t2s[...]
        arrive(t2g.at[pl.ds(0, s.kh - 1)], rsem.at[11])

    @pl.when(jnp.logical_not(mine))
    def _():
        arrive(t2g, rsem.at[11])

    right2 = t2g[...].reshape(s.dh, s.fb)

    def back(q, _):
        prod = jnp.dot(vv[q].reshape(s.fb, s.dh), right2, preferred_element_type=F32)
        prod = prod * (2.0 / s.n)
        sp[q] = prod
        sp_out[q] = prod.astype(BF16)
        send(sp_out.at[q], sp_in.at[q], ssem.at[16], rsem.at[12], mate, z)
        return 0

    lax.fori_loop(0, s.nz, back, 0)
    arrive(sp_in, rsem.at[12])
    for q in range(s.nz):
        sens[q] = (sp[q] + sp_in[q].astype(F32)).astype(BF16)

    x_ring.step(s.hops, every)

    def last(m, _):
        rows = pl.ds(pl.multiple_of(m * s.chunk, s.chunk), s.chunk)
        res = acc[rows, :]
        for q in range(s.nz):
            res += jnp.dot(xa[q, rows, :], sens[q], preferred_element_type=F32)
        out_ref[rows, :] = res.astype(BF16)
        return 0

    lax.fori_loop(0, CHUNKS, last, 0)

    g_ring.drain()
    x_ring.drain()
    arrive(pad, ssem.at[0])
    arrive(m_in.at[pl.ds(0, s.nr - 1)], ssem.at[1])
    arrive(grid.at[0, 0, pl.ds(0, s.nz - 1)], ssem.at[2])
    arrive(mean.at[pl.ds(0, s.nz - 1)], ssem.at[3])
    arrive(grid.at[0, pl.ds(0, s.nx - 1)], ssem.at[4])
    arrive(grid.at[pl.ds(0, s.ny - 1)], ssem.at[5])
    arrive(vv.at[:, c], ssem.at[6])
    arrive(t1s, ssem.at[8])
    arrive(c128.at[c, pl.ds(0, s.nz - 1), pl.ds(0, early)], ssem.at[9])
    arrive(c128.at[c, pl.ds(0, s.nz - 1), pl.ds(0, s.nz - 1 - early)], ssem.at[10])
    arrive(c128.at[c, pl.ds(0, s.nz - 1), pl.ds(0, 1)], ssem.at[11])
    arrive(c128.at[c], ssem.at[12])
    arrive(t2p, ssem.at[14])
    arrive(part.at[pl.ds(0, s.nk - 1)], ssem.at[15])
    arrive(sp_out, ssem.at[16])
    for h in range(s.hops + 1):
        n = len(round_of(h))
        arrive(cp_in.at[pl.ds(0, n)], ds_.at[h])
        arrive(part_in.at[pl.ds(0, s.nk - 1), pl.ds(0, n)], rs_.at[h])


def local(features, grad_out, eigvecs, eigvals, whiten):
    tok, fb = features.shape
    s = Dims(lax.axis_size("rows"), lax.axis_size("feat"), tok * lax.axis_size("rows"), whiten.shape[0])
    dma = pltpu.SemaphoreType.DMA
    vmem = pltpu.VMEM
    vm = pl.BlockSpec(memory_space=pltpu.VMEM)
    return pl.pallas_call(
        functools.partial(whole_kernel, s),
        name="whole",
        out_shape=jax.ShapeDtypeStruct((tok, fb), BF16),
        in_specs=[vm] * 5,
        out_specs=vm,
        scratch_shapes=[
            vmem((s.nz, tok, fb), BF16),
            vmem((s.nz, tok, fb), BF16),
            vmem((s.ny, s.nx, s.nz, s.fbh, s.ea), BF16),
            vmem((s.nz, 2, s.fbh, s.dh), BF16),
            vmem((s.fb, s.ea), BF16),
            vmem((s.fb, s.ea), BF16),
            vmem((s.fb, s.ea), BF16),
            vmem((1, 1, 2 * s.fb), F32),
            vmem((s.nr, 1, 2 * s.fb), F32),
            vmem((s.nz, 1, 2 * s.fb), F32),
            vmem((fb, tok), BF16),
            vmem((tok, fb), F32),
            vmem((s.ea, s.dh), F32),
            vmem((s.nz, 2, s.fb, s.fbh), F32),
            vmem((s.nz, s.fb, s.fbh), F32),
            vmem((s.nk, s.nz, s.sr, s.fbh), BF16),
            vmem((s.nk, s.nz, s.sr, s.fbh), BF16),
            vmem((2, s.nz, s.nz, s.sr, s.fbh), BF16),
            vmem((s.kh, s.nz, s.sr, s.ea), BF16),
            vmem((s.nz, s.nk, s.sr, s.ea), BF16),
            vmem((s.ea, s.dh), F32),
            vmem((s.kh, s.ea, s.ea), BF16),
            vmem((s.kh, s.ea, s.ea), BF16),
            vmem((s.ea, s.fb), F32),
            vmem((s.ea, s.fb), F32),
            vmem((2, s.ea // 2, s.fb), BF16),
            vmem((s.kh, 2, s.ea // 2, s.fb), BF16),
            vmem((s.nz, s.fb, s.fb), F32),
            vmem((s.nz, s.fb, s.fb), BF16),
            vmem((s.nz, s.fb, s.fb), BF16),
            vmem((s.nz, s.fb, s.fb), BF16),
            dma((17,)),
            dma((13,)),
            dma((s.ny,)),
            dma,
            dma((2,)),
            dma((2,)),
            dma((2, s.hops, CHUNKS)),
            dma((2,)),
            dma((2,)),
            dma((2, s.hops, CHUNKS)),
            dma((s.hops + 1,)),
            dma((s.hops + 1,)),
            dma((s.hops + 1,)),
            dma((s.hops + 1,)),
            dma((3,)),
        ],
        compiler_params=pltpu.CompilerParams(
            collective_id=0, has_side_effects=True, vmem_limit_bytes=VMEM_CAP
        ),
        cost_estimate=pl.CostEstimate(flops=60_000_000_000, bytes_accessed=16_000_000, transcendentals=0),
    )(features, grad_out, eigvecs, eigvals.reshape(s.nk, 1, s.ea), whiten.reshape(s.nz, s.fb, fb))


def solution(mesh):
    in_specs = (P("rows", "feat"), P("rows", "feat"), P("feat", "rows"), P(), P(None, "feat"))
    out_specs = P("rows", "feat")
    return jax.shard_map(local, mesh=mesh, in_specs=in_specs, out_specs=out_specs, check_vma=False)
```

time: 159 us -> 127 us (0.80)
  Pallas kernels: 141 us -> 123 us
  between operations: 13.5 us -> 0.01 us
  local copies, waits for them, and re-layouts: 1.69 us -> 3.46 us
    pallas_call x3 -> x1, Pallas kernels: 141 us -> 123 us  [local(): pl.pallas_call(functools.partial(whole_kernel, s), name='whole', out_shap...]
    unnamed x3 -> x2, local copies, waits for them, and re-layouts: 1.6 us -> 3.46 us
  transfers between devices with their start and end apart: 2 -> 0, of which waited for: 1 -> 0; matrix products, arithmetic and copies ran while one was open for 2% -> 0% of each run, Pallas kernels for 84% -> 0%
where the time goes in v2:
time: 127 us
  Pallas kernels  123 us (97%)
  local copies, waits for them, and re-layouts  3.46 us (3%)
    pallas_call x1, Pallas kernels, local(): pl.pallas_call(functools.partial(whole_kernel, s), name='whole', out_shap...  123 us
    unnamed x2, local copies, waits for them, and re-layouts  3.46 us

profile of v2, /device:TPU:1, one launch (start us, length us, event | category | flops | bytes accessed | tf_op | source)
XLA Modules:
  0.0 126.9 jit_solution(12024857224738449299)
XLA Ops:
  0.0 1.6 %copy.6.v_ref = f32[256,64]{1,0:T(8,128)} copy(f32[256,64]{0,1:T(8,128)} %param.7) | data formatting | bytes 131072 | tf_op args[2]
  1.6 123.5 %whole.1 = bf16[1024,256]{1,0:T(8,128)(2,1)} custom-call(bf16[1024,256]{1,0:T(8,128)(2,1)} %x_ref.1, bf16[1024,256]{1,0:T(8,128)(2,1)} %g_ref.1, f32[256,64]{1,0:T(8,128)} %copy.6.v_ref, f32[16,1,128]{2,1,0:T(1,128)} %bitcast.3, bf16[8,256,256]{2,1,0:T(8,128)(2,1)} %bitcast.2), custom_call_target="tpu_custom_call" | custom-call | flops 60000002048 | bytes 16000000 | tf_op jit(solution)/shard_map/whole/pallas_call | solution.py:493
  125.1 1.9 %copy.8 = bf16[1024,256]{1,0:T(8,128)(2,1)} copy(bf16[1024,256]{1,0:T(8,128)(2,1)} %whole.1) | data formatting | bytes 1048576

commit v3 on v2

--- a/solution.py
+++ b/solution.py
@@ -75,7 +75,7 @@
 
     lax.fori_loop(1, s.nr, plane, 0)
     lax.fori_loop(1, s.nz, line, 0)
-    pl.semaphore_wait(barrier, s.nr - 1 + s.nz - 1)
+    return lambda: pl.semaphore_wait(barrier, s.nr - 1 + s.nz - 1)
 
 
 class Ring:
@@ -122,12 +122,41 @@
             arrive(self.buf.at[0, pl.ds(0, s.tok // 2)], self.hsem.at[way])
 
 
+class Axis:
+    def __init__(self, n, pos, device, z, block, part, ssem, rsem):
+        self.n, self.pos, self.device, self.z = n, pos, device, z
+        self.block, self.part, self.ssem, self.rsem = block, part, ssem, rsem
+        self.right = lax.rem(pos + 1, n)
+        self.left = lax.rem(pos + n - 1, n)
+        self.far = lax.rem(pos + 2, n)
+
+    def put(self, ref, sem, to):
+        send(ref, ref, self.ssem, self.rsem.at[sem], self.device(to), self.z)
+
+    def start(self):
+        self.put(self.block(self.pos), 0, self.right)
+        if self.n > 2:
+            self.put(self.block(self.pos), 1, self.left)
+
+    def forward(self):
+        arrive(self.block(0), self.rsem.at[0])
+        if self.n > 2:
+            self.put(self.part(self.left, 0), 2, self.right)
+            arrive(self.block(0), self.rsem.at[1])
+            self.put(self.part(self.right, 1), 3, self.left)
+
+    def finish(self):
+        if self.n > 2:
+            arrive(self.part(0, 0), self.rsem.at[2])
+            arrive(self.part(0, 1), self.rsem.at[3])
+
+
 def whole_kernel(
-    s, x_ref, g_ref, v_ref, e_ref, w_ref, out_ref,
-    ga, xa, grid, vv, pad, pad_in, tile, m_out, m_in, mean, xct, acc, kk_buf,
+    s, x_hbm, g_hbm, v_ref, e_ref, w_hbm, out_ref,
+    x_ref, g_ref, w_ref, ga, xa, grid, vv, pad, pad_in, tile, m_out, m_in, mean, xct, acc, kk_buf,
     cp, cp_in, part, part_in, c128, t1s, t1r, mt, sy_out, sy_in, t2p, t2d, t2s, t2g,
     sp, sp_out, sp_in, sens,
-    ssem, rsem, p2sem, lsem, gs, gh, gr, xs, xh, xr, ds_, dr_, rs_, rr_, zr_,
+    ssem, rsem, asem, bsem, lsem, isem, gs, gh, gr, xs, xh, xr, ds_, dr_, rs_, rr_, zr_,
 ):
     r, z, k, c = where_am_i()
     y, x = k // s.nx, lax.rem(k, s.nx)
@@ -142,16 +171,25 @@
     g_ring = Ring(s, r, z, g_ref, ga, gs, gh, gr)
     x_ring = Ring(s, r, z, xa.at[z], xa, xs, xh, xr)
 
-    v = v_ref[...]
+    welcome = greet(s, r, z)
+    loads = [
+        pltpu.make_async_copy(src, dst, isem.at[i])
+        for i, (src, dst) in enumerate(((g_hbm, g_ref), (x_hbm, x_ref), (w_hbm, w_ref)))
+    ]
+    for load in loads:
+        load.start()
+    v = v_ref[...].T
     twice = jnp.concatenate([v, v], axis=1)
     lane_half = lax.broadcasted_iota(jnp.int32, twice.shape, 1) // s.er
     pad[...] = jnp.where(lane_half == c, twice, 0.0).astype(BF16)
+    loads[0].wait()
+    loads[1].wait()
     sum_x = jnp.sum(x_ref[...].astype(F32), axis=0, keepdims=True)
     sum_g = jnp.sum(g_ref[...].astype(F32), axis=0, keepdims=True)
     m_out[0] = jnp.concatenate([sum_x, sum_g], axis=1)
     m_in[r] = m_out[0]
 
-    greet(s, r, z)
+    welcome()
 
     send(pad, pad_in, ssem.at[0], rsem.at[0], mate, z)
     g_ring.begin([0])
@@ -170,8 +208,16 @@
         return 0
 
     lax.fori_loop(1, s.nz, up, 0)
-    g_ring.begin(every[1:])
+    g_ring.begin([1])
     ga[z] = g_ref[...]
+
+    s_row = jnp.broadcast_to(lax.rsqrt(e_ref[k]), (s.ea, s.ea)).T
+    for j in range(s.kh):
+        s_col = lax.rsqrt(e_ref[c * s.kh + j])
+        both = s_row * s_col
+        kk_buf[:, j * s.ea : (j + 1) * s.ea] = -(both * both) / (s_row + s_col)
+    acc[...] = jnp.zeros_like(acc)
+    loads[2].wait()
 
     arrive(m_in.at[pl.ds(0, s.nr - 1)], rsem.at[1])
     own_mean = jnp.sum(m_in[...], axis=0) / s.n
@@ -182,11 +228,11 @@
         return 0
 
     lax.fori_loop(1, s.nz, mean_up, 0)
+    g_ring.begin([2, 3])
     centered = (x_ref[...].astype(F32) - own_mean[:, : s.fb]).astype(BF16)
     xa[z] = centered
     xct[...] = centered.astype(F32).T.astype(BF16)
     col_sum = jnp.sum(xct[...].astype(F32), axis=1, keepdims=True)
-    acc[...] = jnp.zeros_like(acc)
 
     def gram(slot, blk):
         nu = mean[blk][:, s.fb :]
@@ -247,26 +293,21 @@
         lax.fori_loop(1, s.nz, lift, 0)
         return slots
 
-    arrive(mean.at[pl.ds(0, s.nz - 1)], rsem.at[3])
-    round_start(0)
-
-    arrive(grid.at[0, 0, pl.ds(0, s.nz - 1)], rsem.at[2])
-
-    def along_a(t, _):
-        a2 = lax.rem(a + t, s.nx)
-        y2, x2 = jnp.where(first, y, a2), jnp.where(first, a2, x)
-        send(grid.at[b, a], grid.at[b, a], ssem.at[4], rsem.at[4], (y2 * s.nx + x2) * 2 + c, z)
-        return 0
-
-    lax.fori_loop(1, s.nx, along_a, 0)
-    round_scatter(0)
-    product(z)
-
-    def along_b(t, _):
-        b2 = lax.rem(b + t, s.ny)
-        y2, x2 = jnp.where(first, b2, y), jnp.where(first, x, b2)
-        send(grid.at[b], grid.at[b], ssem.at[5], p2sem.at[t], (y2 * s.nx + x2) * 2 + c, z)
-        return 0
+    assert s.nx == s.ny and s.nx in (2, 4)
+    nzh, nxh = s.nz // 2, s.nx // 2
+
+    def device(a2, b2):
+        y2, x2 = jnp.where(first, b2, a2), jnp.where(first, a2, b2)
+        return (y2 * s.nx + x2) * 2 + c
+
+    axis_a = Axis(
+        s.nx, a, lambda p: device(p, b), z, lambda p: grid.at[b, p],
+        lambda p, i: grid.at[b, p, pl.ds(i * nzh, nzh)], ssem.at[4], asem,
+    )
+    axis_b = Axis(
+        s.ny, b, lambda p: device(a, p), z, lambda p: grid.at[p],
+        lambda p, i: grid.at[p, pl.ds(i * nxh, nxh)], ssem.at[5], bsem,
+    )
 
     def hand_out(b2):
         def each(a2, _):
@@ -288,41 +329,49 @@
 
         lax.fori_loop(0, s.nx, each, 0)
 
-    arrive(grid.at[0, pl.ds(0, s.nx - 1)], rsem.at[4])
-    lax.fori_loop(1, s.ny, along_b, 0)
-    g_ring.step(1, every)
+    arrive(grid.at[0, 0, pl.ds(0, s.nz - 1)], rsem.at[2])
+    axis_a.start()
+    g_ring.step(1, every[:2])
+    arrive(mean.at[pl.ds(0, s.nz - 1)], rsem.at[3])
+    axis_a.forward()
+    round_start(0)
+    g_ring.step(1, every[2:3])
+    axis_a.finish()
+    axis_b.start()
+    round_scatter(0)
+    g_ring.step(1, every[3:])
     hand_out(b)
-
-    s_row = jnp.broadcast_to(lax.rsqrt(e_ref[k]), (s.ea, s.ea)).T
-    for j in range(s.kh):
-        s_col = lax.rsqrt(e_ref[c * s.kh + j])
-        both = s_row * s_col
-        kk_buf[:, j * s.ea : (j + 1) * s.ea] = -(both * both) / (s_row + s_col)
 
     for h in range(1, s.hops):
         round_start(h)
+        for _, blk in round_of(h - 1):
+            product(blk)
         round_scatter(h)
+        if h == s.hops - 2:
+            axis_b.forward()
+            hand_out(axis_b.left)
+            if s.ny > 2:
+                hand_out(axis_b.right)
+        if h == s.hops - 1:
+            g_ring.step(h + 1, every[:1])
+            round_sum(range(0, h), 0)
+            g_ring.step(h + 1, every[1:])
+        else:
+            g_ring.step(h + 1, every)
+
+    round_start(s.hops)
+    x_ring.begin([0])
+    round_scatter(s.hops)
+    round_sum([s.hops - 1], 1)
+    for h in (s.hops - 1, s.hops):
         for _, blk in round_of(h):
             product(blk)
-        if h == s.hops - 1:
-            round_sum(range(0, h), 0)
-        g_ring.step(h + 1, every)
-
-    round_start(s.hops)
-    x_ring.begin(every[: CHUNKS // 2])
-    round_scatter(s.hops)
-    product(round_of(s.hops)[0][1])
-
-    def landed(t, _):
-        b2 = lax.rem(b + s.ny - t, s.ny)
-        arrive(grid.at[b2], p2sem.at[t])
-        hand_out(b2)
-        return 0
-
-    lax.fori_loop(1, s.ny, landed, 0)
-    round_sum([s.hops - 1], 1)
+
     round_sum([s.hops], 2)
-    x_ring.begin(every[CHUNKS // 2 :])
+    x_ring.begin(every[1:])
+    axis_b.finish()
+    if s.ny > 2:
+        hand_out(axis_b.far)
 
     early = round_of(s.hops - 2)[-1][0] + 1
     arrive(c128.at[c, pl.ds(0, s.nz - 1), pl.ds(0, early)], zr_.at[0])
@@ -338,27 +387,29 @@
             bands.append(jnp.concatenate([c128[h, src, s.slot(src, g)] for g in range(s.nz)], axis=1))
         return jnp.concatenate(bands, axis=0)
 
-    def basis_rows(h):
-        return vv[:, h].reshape(s.dh, s.dh)
-
-    t1 = jnp.dot(cross_rows(c), basis_rows(c), preferred_element_type=F32)
+    crosses = [cross_rows(c)]
     arrive(c128.at[1 - c], rsem.at[7])
-    t1 += jnp.dot(cross_rows(1 - c), basis_rows(1 - c), preferred_element_type=F32)
-    for j in range(s.kh):
-        t1s[j] = t1[:, j * s.ea : (j + 1) * s.ea].astype(BF16).reshape(s.nz, s.sr, s.ea)
-
-    def turn(t, _):
-        j = lax.rem(kk + t, s.kh)
-        k2 = c * s.kh + j
-
-        @pl.when(k2 != k)
-        def _():
-            send(t1s.at[j], t1r.at[:, k], ssem.at[7], rsem.at[8], 2 * k2 + c, z)
-
-        send(t1s.at[j], t1r.at[:, k], ssem.at[8], rsem.at[8], 2 * k2 + 1 - c, z)
-        return 0
-
-    lax.fori_loop(0, s.kh, turn, 0)
+    crosses.append(cross_rows(1 - c))
+    for t in range(s.kh // 2):
+        pair = lax.rem(kk // 2 + t, s.kh // 2)
+        cols = pl.ds(pl.multiple_of(pair * 2 * s.ea, 2 * s.ea), 2 * s.ea)
+        t1 = sum(
+            jnp.dot(
+                crosses[i], vv[:, h, :, cols].reshape(s.dh, 2 * s.ea), preferred_element_type=F32
+            )
+            for i, h in enumerate((c, 1 - c))
+        )
+        for i in range(2):
+            j = pair * 2 + i
+            k2 = c * s.kh + j
+            t1s[j] = t1[:, i * s.ea : (i + 1) * s.ea].astype(BF16).reshape(s.nz, s.sr, s.ea)
+
+            @pl.when(k2 != k)
+            def _():
+                send(t1s.at[j], t1r.at[:, k], ssem.at[7], rsem.at[8], 2 * k2 + c, z)
+
+            send(t1s.at[j], t1r.at[:, k], ssem.at[8], rsem.at[8], 2 * k2 + 1 - c, z)
+
     x_ring.step(1, every)
 
     @pl.when(mine)
@@ -388,7 +439,7 @@
         return 0
 
     lax.fori_loop(0, s.kh, mirror, 0)
-    x_ring.step(2, every[: CHUNKS // 2])
+    x_ring.step(2, every[:2])
 
     @pl.when(mine)
     def _():
@@ -413,7 +464,7 @@
         )
     t2p[...] = total
     send(t2p, t2d, ssem.at[14], rsem.at[10], mate, z)
-    x_ring.step(2, every[CHUNKS // 2 :])
+    x_ring.step(2, every[2:])
     arrive(t2d, rsem.at[10])
     t2s[...] = (t2p[...] + t2d[...]).astype(BF16).reshape(t2s.shape)
 
@@ -490,13 +541,17 @@
     dma = pltpu.SemaphoreType.DMA
     vmem = pltpu.VMEM
     vm = pl.BlockSpec(memory_space=pltpu.VMEM)
+    hbm = pl.BlockSpec(memory_space=pl.ANY)
     return pl.pallas_call(
         functools.partial(whole_kernel, s),
         name="whole",
         out_shape=jax.ShapeDtypeStruct((tok, fb), BF16),
-        in_specs=[vm] * 5,
+        in_specs=[hbm, hbm, vm, vm, hbm],
         out_specs=vm,
         scratch_shapes=[
+            vmem((tok, fb), BF16),
+            vmem((tok, fb), BF16),
+            vmem((s.nz, s.fb, fb), BF16),
             vmem((s.nz, tok, fb), BF16),
             vmem((s.nz, tok, fb), BF16),
             vmem((s.ny, s.nx, s.nz, s.fbh, s.ea), BF16),
@@ -530,8 +585,10 @@
             vmem((s.nz, s.fb, s.fb), BF16),
             dma((17,)),
             dma((13,)),
-            dma((s.ny,)),
+            dma((4,)),
+            dma((4,)),
             dma,
+            dma((3,)),
             dma((2,)),
             dma((2,)),
             dma((2, s.hops, CHUNKS)),
@@ -548,7 +605,7 @@
             collective_id=0, has_side_effects=True, vmem_limit_bytes=VMEM_CAP
         ),
         cost_estimate=pl.CostEstimate(flops=60_000_000_000, bytes_accessed=16_000_000, transcendentals=0),
-    )(features, grad_out, eigvecs, eigvals.reshape(s.nk, 1, s.ea), whiten.reshape(s.nz, s.fb, fb))
+    )(features, grad_out, eigvecs.T, eigvals.reshape(s.nk, 1, s.ea), whiten.reshape(s.nz, s.fb, fb))
 
 
 def solution(mesh):

time: 127 us -> 113 us (0.89)
  Pallas kernels: 123 us -> 111 us
  local copies, waits for them, and re-layouts: 3.46 us -> 1.87 us
    pallas_call x1, Pallas kernels: 123 us -> 111 us  [local(): pl.pallas_call(functools.partial(whole_kernel, s), name='whole', out_shap...]
    unnamed x2 -> x1, local copies, waits for them, and re-layouts: 3.46 us -> 1.87 us
where the time goes in v3:
time: 113 us
  Pallas kernels  111 us (98%)
  local copies, waits for them, and re-layouts  1.87 us (2%)
    pallas_call x1, Pallas kernels, local(): pl.pallas_call(functools.partial(whole_kernel, s), name='whole', out_shap...  111 us

profile of v3, /device:TPU:1, one launch (start us, length us, event | category | flops | bytes accessed | tf_op | source)
XLA Modules:
  0.0 112.9 jit_solution(11822086889063388948)
XLA Ops:
  0.0 111.1 %whole.1 = bf16[1024,256]{1,0:T(8,128)(2,1)} custom-call(bf16[1024,256]{1,0:T(8,128)(2,1)} %x_hbm.1, bf16[1024,256]{1,0:T(8,128)(2,1)} %g_hbm.1, f32[64,256]{1,0:T(8,128)} %bitcast.4, f32[16,1,128]{2,1,0:T(1,128)} %bitcast.5, bf16[8,256,256]{2,1,0:T(8,128)(2,1)} %bitcast.3), custom_call_target="tpu_custom_call" | custom-call | flops 60000002048 | bytes 16000000 | tf_op jit(solution)/shard_map/whole/pallas_call | solution.py:545
  111.1 1.9 %copy.7 = bf16[1024,256]{1,0:T(8,128)(2,1)} copy(bf16[1024,256]{1,0:T(8,128)(2,1)} %whole.1) | data formatting | bytes 1048576

commit v4 on v3

--- a/solution.py
+++ b/solution.py
@@ -11,7 +11,8 @@
 F32 = jnp.float32
 BF16 = jnp.bfloat16
 VMEM_CAP = 62 * 1024 * 1024
-CHUNKS = 4
+CHUNKS = 8
+ROW_TILES = 2
 
 
 class Dims:
@@ -30,7 +31,6 @@
         self.ea = d // self.nk
         self.er = d // rows
         self.hops = feat // 2
-        self.chunk = self.tok // CHUNKS
 
     def slot(self, src, g):
         dist = (g - src) % self.nz
@@ -79,17 +79,24 @@
 
 
 class Ring:
-    def __init__(self, s, r, z, own, buf, ssem, hsem, rsem):
+    def __init__(self, s, r, z, own, buf, chunks, ssem, hsem, rsem):
         self.s, self.r, self.z = s, r, z
-        self.own, self.buf = own, buf
+        self.own, self.buf, self.chunks = own, buf, chunks
+        self.size = buf.shape[1] // chunks
         self.ssem, self.hsem, self.rsem = ssem, hsem, rsem
+        self.done = set()
+
+    def new(self, h, qs):
+        fresh = [q for q in qs if (h, q) not in self.done]
+        self.done.update((h, q) for q in fresh)
+        return fresh
 
     def block(self, way, h):
         nz = self.s.nz
         return lax.rem(self.z + (nz - h if way == 0 else h), nz)
 
     def rows(self, q):
-        return pl.ds(q * self.s.chunk, self.s.chunk)
+        return pl.ds(q * self.size, self.size)
 
     def start(self, way, h, q):
         s = self.s
@@ -97,29 +104,28 @@
         blk = self.block(way, h - 1)
         src = self.own.at[self.rows(q)] if h == 1 else self.buf.at[blk, self.rows(q)]
         ss = self.hsem if h == s.hops else self.ssem
-        send(src, self.buf.at[blk, self.rows(q)], ss.at[way], self.rsem.at[way, h - 1, q], self.r, to)
+        send(src, self.buf.at[blk, self.rows(q)], ss.at[way], self.rsem.at[h - 1, q], self.r, to)
 
     def has(self, way, h, q):
-        return h < self.s.hops or (q < CHUNKS // 2) == (way == 0)
+        return h < self.s.hops or (q < self.chunks // 2) == (way == 0)
 
     def begin(self, qs):
-        for q in qs:
+        for q in self.new(0, qs):
             for way in (0, 1):
                 self.start(way, 1, q)
 
     def step(self, h, qs):
-        for q in qs:
-            for way in (0, 1):
-                if self.has(way, h, q):
-                    arrive(self.buf.at[0, self.rows(q)], self.rsem.at[way, h - 1, q])
-                    if h < self.s.hops and self.has(way, h + 1, q):
-                        self.start(way, h + 1, q)
+        for q in self.new(h, qs):
+            ways = [way for way in (0, 1) if self.has(way, h, q)]
+            arrive(self.buf.at[0, pl.ds(0, len(ways) * self.size)], self.rsem.at[h - 1, q])
+            for way in ways:
+                if h < self.s.hops and self.has(way, h + 1, q):
+                    self.start(way, h + 1, q)
 
     def drain(self):
-        s = self.s
         for way in (0, 1):
-            arrive(self.buf.at[pl.ds(0, s.hops - 1)], self.ssem.at[way])
-            arrive(self.buf.at[0, pl.ds(0, s.tok // 2)], self.hsem.at[way])
+            arrive(self.buf.at[pl.ds(0, self.s.hops - 1)], self.ssem.at[way])
+            arrive(self.buf.at[0, pl.ds(0, self.buf.shape[1] // 2)], self.hsem.at[way])
 
 
 class Axis:
@@ -152,11 +158,11 @@
 
 
 def whole_kernel(
-    s, x_hbm, g_hbm, v_ref, e_ref, w_hbm, out_ref,
-    x_ref, g_ref, w_ref, ga, xa, grid, vv, pad, pad_in, tile, m_out, m_in, mean, xct, acc, kk_buf,
+    s, x_hbm, g_hbm, v_hbm, e_hbm, w_hbm, out_ref,
+    x_ref, g_ref, v_ref, e_ref, w_ref, ga, xa, grid, vv, pad, pad_in, tile, m_out, m_in, mean, xct, acc, kk_buf,
     cp, cp_in, part, part_in, c128, t1s, t1r, mt, sy_out, sy_in, t2p, t2d, t2s, t2g,
     sp, sp_out, sp_in, sens,
-    ssem, rsem, asem, bsem, lsem, isem, gs, gh, gr, xs, xh, xr, ds_, dr_, rs_, rr_, zr_,
+    ssem, rsem, asem, bsem, bfar, lsem, isem, gs, gh, gr, xs, xh, xr, vs, vh, vr, ds_, dr_, rs_, rr_, zr_,
 ):
     r, z, k, c = where_am_i()
     y, x = k // s.nx, lax.rem(k, s.nx)
@@ -168,22 +174,25 @@
     mine = half == c
     kk = lax.rem(k, s.kh)
     every = range(CHUNKS)
-    g_ring = Ring(s, r, z, g_ref, ga, gs, gh, gr)
-    x_ring = Ring(s, r, z, xa.at[z], xa, xs, xh, xr)
+    g_ring = Ring(s, r, z, g_ref, ga, CHUNKS, gs, gh, gr)
+    x_ring = Ring(s, r, z, xa.at[z], xa, CHUNKS, xs, xh, xr)
+    v_ring = Ring(s, r, z, grid.at[b, a, z], grid.at[b, a], 2, vs, vh, vr)
 
     welcome = greet(s, r, z)
+    inputs = (v_hbm, v_ref), (g_hbm, g_ref), (x_hbm, x_ref), (e_hbm, e_ref), (w_hbm, w_ref)
     loads = [
         pltpu.make_async_copy(src, dst, isem.at[i])
-        for i, (src, dst) in enumerate(((g_hbm, g_ref), (x_hbm, x_ref), (w_hbm, w_ref)))
+        for i, (src, dst) in enumerate(inputs)
     ]
     for load in loads:
         load.start()
+    loads[0].wait()
     v = v_ref[...].T
     twice = jnp.concatenate([v, v], axis=1)
     lane_half = lax.broadcasted_iota(jnp.int32, twice.shape, 1) // s.er
     pad[...] = jnp.where(lane_half == c, twice, 0.0).astype(BF16)
-    loads[0].wait()
     loads[1].wait()
+    loads[2].wait()
     sum_x = jnp.sum(x_ref[...].astype(F32), axis=0, keepdims=True)
     sum_g = jnp.sum(g_ref[...].astype(F32), axis=0, keepdims=True)
     m_out[0] = jnp.concatenate([sum_x, sum_g], axis=1)
@@ -203,21 +212,20 @@
     tile[...] = pad[...] + pad_in[...]
     grid[b, a, z] = tile[pl.ds(pl.multiple_of(c * s.fbh, s.fbh), s.fbh), :]
 
-    def up(t, _):
-        send(grid.at[b, a, z], grid.at[b, a, z], ssem.at[2], rsem.at[2], r, lax.rem(z + t, s.nz))
-        return 0
-
-    lax.fori_loop(1, s.nz, up, 0)
-    g_ring.begin([1])
+    v_ring.begin([0, 1])
+    g_ring.begin([1, 2, 3])
     ga[z] = g_ref[...]
 
+    loads[3].wait()
     s_row = jnp.broadcast_to(lax.rsqrt(e_ref[k]), (s.ea, s.ea)).T
     for j in range(s.kh):
         s_col = lax.rsqrt(e_ref[c * s.kh + j])
         both = s_row * s_col
         kk_buf[:, j * s.ea : (j + 1) * s.ea] = -(both * both) / (s_row + s_col)
     acc[...] = jnp.zeros_like(acc)
-    loads[2].wait()
+    loads[4].wait()
+    v_ring.step(1, [0, 1])
+    g_ring.begin([4, 5])
 
     arrive(m_in.at[pl.ds(0, s.nr - 1)], rsem.at[1])
     own_mean = jnp.sum(m_in[...], axis=0) / s.n
@@ -228,7 +236,9 @@
         return 0
 
     lax.fori_loop(1, s.nz, mean_up, 0)
-    g_ring.begin([2, 3])
+    if s.hops > 2:
+        v_ring.step(2, [0, 1])
+    g_ring.begin([6, 7])
     centered = (x_ref[...].astype(F32) - own_mean[:, : s.fb]).astype(BF16)
     xa[z] = centered
     xct[...] = centered.astype(F32).T.astype(BF16)
@@ -294,7 +304,7 @@
         return slots
 
     assert s.nx == s.ny and s.nx in (2, 4)
-    nzh, nxh = s.nz // 2, s.nx // 2
+    nzh = s.nz // 2
 
     def device(a2, b2):
         y2, x2 = jnp.where(first, b2, a2), jnp.where(first, a2, b2)
@@ -304,10 +314,33 @@
         s.nx, a, lambda p: device(p, b), z, lambda p: grid.at[b, p],
         lambda p, i: grid.at[b, p, pl.ds(i * nzh, nzh)], ssem.at[4], asem,
     )
-    axis_b = Axis(
-        s.ny, b, lambda p: device(a, p), z, lambda p: grid.at[p],
-        lambda p, i: grid.at[p, pl.ds(i * nxh, nxh)], ssem.at[5], bsem,
-    )
+    b_right, b_left = lax.rem(b + 1, s.ny), lax.rem(b + s.ny - 1, s.ny)
+    b_far = lax.rem(b + 2, s.ny)
+    pieces = [a, axis_a.left] + ([axis_a.right, axis_a.far] if s.nx > 2 else [])
+
+    def put_b(b2, piece, sem, to):
+        ref = grid.at[b2, pieces[piece]]
+        send(ref, ref, ssem.at[5], sem, device(a, to), z)
+
+    def b_start(piece):
+        put_b(b, piece, bsem.at[0, piece], b_right)
+        if s.ny > 2:
+            put_b(b, piece, bsem.at[1, piece], b_left)
+
+    def b_forward():
+        for piece in range(len(pieces)):
+            arrive(grid.at[0, 0], bsem.at[0, piece])
+            if s.ny > 2:
+                if piece % 2 == 0:
+                    put_b(b_left, piece, bfar.at[piece], b_right)
+                arrive(grid.at[0, 0], bsem.at[1, piece])
+                if piece % 2 == 1:
+                    put_b(b_right, piece, bfar.at[piece], b_left)
+
+    def b_finish():
+        if s.ny > 2:
+            for piece in range(len(pieces)):
+                arrive(grid.at[0, 0], bfar.at[piece])
 
     def hand_out(b2):
         def each(a2, _):
@@ -329,49 +362,56 @@
 
         lax.fori_loop(0, s.nx, each, 0)
 
-    arrive(grid.at[0, 0, pl.ds(0, s.nz - 1)], rsem.at[2])
+    if s.hops > 3:
+        v_ring.step(3, [0, 1])
+    g_ring.step(1, every[:4])
+    v_ring.step(s.hops, [0, 1])
     axis_a.start()
-    g_ring.step(1, every[:2])
+    b_start(0)
+    g_ring.step(1, every[4:])
     arrive(mean.at[pl.ds(0, s.nz - 1)], rsem.at[3])
+    round_start(0)
+    g_ring.step(2, every[:3])
     axis_a.forward()
-    round_start(0)
-    g_ring.step(1, every[2:3])
-    axis_a.finish()
-    axis_b.start()
+    b_start(1)
+    if s.nx > 2:
+        b_start(2)
     round_scatter(0)
-    g_ring.step(1, every[3:])
-    hand_out(b)
 
     for h in range(1, s.hops):
         round_start(h)
+        if h < s.hops - 1:
+            g_ring.step(h + 1, every[:4])
+        if h == 1:
+            axis_a.finish()
+            if s.nx > 2:
+                b_start(3)
+            hand_out(b)
         for _, blk in round_of(h - 1):
             product(blk)
         round_scatter(h)
+        if h == s.hops - 1:
+            b_forward()
+            hand_out(b_left)
+            if s.ny > 2:
+                hand_out(b_right)
+        g_ring.step(h + 1, every)
         if h == s.hops - 2:
-            axis_b.forward()
-            hand_out(axis_b.left)
-            if s.ny > 2:
-                hand_out(axis_b.right)
-        if h == s.hops - 1:
-            g_ring.step(h + 1, every[:1])
-            round_sum(range(0, h), 0)
-            g_ring.step(h + 1, every[1:])
-        else:
-            g_ring.step(h + 1, every)
+            x_ring.begin(every[:4])
 
     round_start(s.hops)
-    x_ring.begin([0])
     round_scatter(s.hops)
+    round_sum(range(0, s.hops - 1), 0)
     round_sum([s.hops - 1], 1)
     for h in (s.hops - 1, s.hops):
         for _, blk in round_of(h):
             product(blk)
 
     round_sum([s.hops], 2)
-    x_ring.begin(every[1:])
-    axis_b.finish()
+    x_ring.begin(every)
+    b_finish()
     if s.ny > 2:
-        hand_out(axis_b.far)
+        hand_out(b_far)
 
     early = round_of(s.hops - 2)[-1][0] + 1
     arrive(c128.at[c, pl.ds(0, s.nz - 1), pl.ds(0, early)], zr_.at[0])
@@ -387,17 +427,16 @@
             bands.append(jnp.concatenate([c128[h, src, s.slot(src, g)] for g in range(s.nz)], axis=1))
         return jnp.concatenate(bands, axis=0)
 
-    crosses = [cross_rows(c)]
+    mt[...] = jnp.dot(
+        cross_rows(c), vv[:, c].reshape(s.dh, s.dh), preferred_element_type=F32
+    )
     arrive(c128.at[1 - c], rsem.at[7])
-    crosses.append(cross_rows(1 - c))
+    other = cross_rows(1 - c)
     for t in range(s.kh // 2):
         pair = lax.rem(kk // 2 + t, s.kh // 2)
         cols = pl.ds(pl.multiple_of(pair * 2 * s.ea, 2 * s.ea), 2 * s.ea)
-        t1 = sum(
-            jnp.dot(
-                crosses[i], vv[:, h, :, cols].reshape(s.dh, 2 * s.ea), preferred_element_type=F32
-            )
-            for i, h in enumerate((c, 1 - c))
+        t1 = mt[:, cols] + jnp.dot(
+            other, vv[:, 1 - c, :, cols].reshape(s.dh, 2 * s.ea), preferred_element_type=F32
         )
         for i in range(2):
             j = pair * 2 + i
@@ -439,7 +478,7 @@
         return 0
 
     lax.fori_loop(0, s.kh, mirror, 0)
-    x_ring.step(2, every[:2])
+    x_ring.step(2, every[:4])
 
     @pl.when(mine)
     def _():
@@ -464,7 +503,7 @@
         )
     t2p[...] = total
     send(t2p, t2d, ssem.at[14], rsem.at[10], mate, z)
-    x_ring.step(2, every[2:])
+    x_ring.step(2, every[4:])
     arrive(t2d, rsem.at[10])
     t2s[...] = (t2p[...] + t2d[...]).astype(BF16).reshape(t2s.shape)
 
@@ -474,7 +513,7 @@
         return 0
 
     lax.fori_loop(1, s.nk, spread, 0)
-    x_ring.step(3, every)
+    x_ring.step(3, every[:6])
 
     @pl.when(mine)
     def _():
@@ -488,35 +527,51 @@
     right2 = t2g[...].reshape(s.dh, s.fb)
 
     def back(q, _):
-        prod = jnp.dot(vv[q].reshape(s.fb, s.dh), right2, preferred_element_type=F32)
-        prod = prod * (2.0 / s.n)
-        sp[q] = prod
-        sp_out[q] = prod.astype(BF16)
-        send(sp_out.at[q], sp_in.at[q], ssem.at[16], rsem.at[12], mate, z)
-        return 0
-
-    lax.fori_loop(0, s.nz, back, 0)
+        two = pl.ds(2 * q, 2)
+        left2 = vv[two].reshape(2 * s.fb, s.dh)
+        prod = jnp.dot(left2, right2, preferred_element_type=F32) * (2.0 / s.n)
+        prod = prod.reshape(2, s.fb, s.fb)
+        sp[two] = prod
+        sp_out[two] = prod.astype(BF16)
+        send(sp_out.at[two], sp_in.at[two], ssem.at[16], rsem.at[12], mate, z)
+        return 0
+
+    lax.fori_loop(0, s.nz // 4, back, 0)
+    x_ring.step(3, every[6:])
+    lax.fori_loop(s.nz // 4, s.nz // 2, back, 0)
     arrive(sp_in, rsem.at[12])
     for q in range(s.nz):
         sens[q] = (sp[q] + sp_in[q].astype(F32)).astype(BF16)
 
-    x_ring.step(s.hops, every)
-
-    def last(m, _):
-        rows = pl.ds(pl.multiple_of(m * s.chunk, s.chunk), s.chunk)
+    far = x_ring.block(0, s.hops)
+    tile_rows = x_ref.shape[0] // ROW_TILES
+
+    def most(m, _):
+        rows = pl.ds(pl.multiple_of(m * tile_rows, tile_rows), tile_rows)
         res = acc[rows, :]
         for q in range(s.nz):
-            res += jnp.dot(xa[q, rows, :], sens[q], preferred_element_type=F32)
+            if q != s.hops:
+                blk = lax.rem(z + q, s.nz)
+                res += jnp.dot(xa[blk, rows, :], sens[blk], preferred_element_type=F32)
+        acc[rows, :] = res
+        return 0
+
+    lax.fori_loop(0, ROW_TILES, most, 0)
+    x_ring.step(s.hops, every)
+
+    def last(m, _):
+        rows = pl.ds(pl.multiple_of(m * tile_rows, tile_rows), tile_rows)
+        res = acc[rows, :] + jnp.dot(xa[far, rows, :], sens[far], preferred_element_type=F32)
         out_ref[rows, :] = res.astype(BF16)
         return 0
 
-    lax.fori_loop(0, CHUNKS, last, 0)
+    lax.fori_loop(0, ROW_TILES, last, 0)
 
     g_ring.drain()
     x_ring.drain()
     arrive(pad, ssem.at[0])
     arrive(m_in.at[pl.ds(0, s.nr - 1)], ssem.at[1])
-    arrive(grid.at[0, 0, pl.ds(0, s.nz - 1)], ssem.at[2])
+    v_ring.drain()
     arrive(mean.at[pl.ds(0, s.nz - 1)], ssem.at[3])
     arrive(grid.at[0, pl.ds(0, s.nx - 1)], ssem.at[4])
     arrive(grid.at[pl.ds(0, s.ny - 1)], ssem.at[5])
@@ -545,12 +600,14 @@
     return pl.pallas_call(
         functools.partial(whole_kernel, s),
         name="whole",
-        out_shape=jax.ShapeDtypeStruct((tok, fb), BF16),
-        in_specs=[hbm, hbm, vm, vm, hbm],
+        out_shape=pltpu.VMEM((tok, fb), BF16),
+        in_specs=[hbm] * 5,
         out_specs=vm,
         scratch_shapes=[
             vmem((tok, fb), BF16),
             vmem((tok, fb), BF16),
+            vmem((s.er, s.fb), F32),
+            vmem((s.nk, 1, s.ea), F32),
             vmem((s.nz, s.fb, fb), BF16),
             vmem((s.nz, tok, fb), BF16),
             vmem((s.nz, tok, fb), BF16),
@@ -586,15 +643,19 @@
             dma((17,)),
             dma((13,)),
             dma((4,)),
+            dma((2, 4)),
             dma((4,)),
             dma,
-            dma((3,)),
+            dma((5,)),
             dma((2,)),
             dma((2,)),
-            dma((2, s.hops, CHUNKS)),
+            dma((s.hops, CHUNKS)),
             dma((2,)),
             dma((2,)),
-            dma((2, s.hops, CHUNKS)),
+            dma((s.hops, CHUNKS)),
+            dma((2,)),
+            dma((2,)),
+            dma((s.hops, 2)),
             dma((s.hops + 1,)),
             dma((s.hops + 1,)),
             dma((s.hops + 1,)),

time: 113 us -> 103 us (0.912)
  Pallas kernels: 111 us -> 102 us
    pallas_call x1, Pallas kernels: 111 us -> 102 us  [local(): pl.pallas_call(functools.partial(whole_kernel, s), name='whole', out_shap...]
where the time goes in v4:
time: 103 us
  Pallas kernels  102 us (99%)
    pallas_call x1, Pallas kernels, local(): pl.pallas_call(functools.partial(whole_kernel, s), name='whole', out_shap...  102 us

profile of v4, /device:TPU:1, one launch (start us, length us, event | category | flops | bytes accessed | tf_op | source)
XLA Modules:
  0.0 103.3 jit_solution(6378381601131703571)
XLA Ops:
  0.0 102.5 %whole.1 = bf16[1024,256]{1,0:T(8,128)(2,1)S(1)} custom-call(bf16[1024,256]{1,0:T(8,128)(2,1)} %x_hbm.1, bf16[1024,256]{1,0:T(8,128)(2,1)} %g_hbm.1, f32[64,256]{1,0:T(8,128)} %bitcast.4, f32[16,1,128]{2,1,0:T(1,128)} %bitcast.5, bf16[8,256,256]{2,1,0:T(8,128)(2,1)} %bitcast.3), custom_call_target="tpu_custom_call" | custom-call | flops 60000002048 | bytes 16000000 | tf_op jit(solution)/shard_map/whole/pallas_call | solution.py:600
  102.5 0.8 copy.7

commit v5 on v4

--- a/solution.py
+++ b/solution.py
@@ -79,10 +79,9 @@
 
 
 class Ring:
-    def __init__(self, s, r, z, own, buf, chunks, ssem, hsem, rsem):
+    def __init__(self, s, r, z, own, buf, cuts, ssem, hsem, rsem):
         self.s, self.r, self.z = s, r, z
-        self.own, self.buf, self.chunks = own, buf, chunks
-        self.size = buf.shape[1] // chunks
+        self.own, self.buf, self.cuts = own, buf, cuts
         self.ssem, self.hsem, self.rsem = ssem, hsem, rsem
         self.done = set()
 
@@ -96,7 +95,7 @@
         return lax.rem(self.z + (nz - h if way == 0 else h), nz)
 
     def rows(self, q):
-        return pl.ds(q * self.size, self.size)
+        return pl.ds(*self.cuts[q])
 
     def start(self, way, h, q):
         s = self.s
@@ -107,7 +106,7 @@
         send(src, self.buf.at[blk, self.rows(q)], ss.at[way], self.rsem.at[h - 1, q], self.r, to)
 
     def has(self, way, h, q):
-        return h < self.s.hops or (q < self.chunks // 2) == (way == 0)
+        return h < self.s.hops or (q < len(self.cuts) // 2) == (way == 0)
 
     def begin(self, qs):
         for q in self.new(0, qs):
@@ -117,15 +116,23 @@
     def step(self, h, qs):
         for q in self.new(h, qs):
             ways = [way for way in (0, 1) if self.has(way, h, q)]
-            arrive(self.buf.at[0, pl.ds(0, len(ways) * self.size)], self.rsem.at[h - 1, q])
+            both = pl.ds(0, len(ways) * self.cuts[q][1])
+            arrive(self.buf.at[0, both], self.rsem.at[h - 1, q])
             for way in ways:
                 if h < self.s.hops and self.has(way, h + 1, q):
                     self.start(way, h + 1, q)
 
     def drain(self):
-        for way in (0, 1):
-            arrive(self.buf.at[pl.ds(0, self.s.hops - 1)], self.ssem.at[way])
-            arrive(self.buf.at[0, pl.ds(0, self.buf.shape[1] // 2)], self.hsem.at[way])
+        sizes = [size for _, size in self.cuts]
+        half = len(sizes) // 2
+        for way, far in ((0, sum(sizes[:half])), (1, sum(sizes[half:]))):
+            near = self.buf.at[pl.ds(0, self.s.hops - 1), pl.ds(0, sum(sizes))]
+            arrive(near, self.ssem.at[way])
+            arrive(self.buf.at[0, pl.ds(0, far)], self.hsem.at[way])
+
+
+def even(length, parts):
+    return [(i * length // parts, length // parts) for i in range(parts)]
 
 
 class Axis:
@@ -162,7 +169,7 @@
     x_ref, g_ref, v_ref, e_ref, w_ref, ga, xa, grid, vv, pad, pad_in, tile, m_out, m_in, mean, xct, acc, kk_buf,
     cp, cp_in, part, part_in, c128, t1s, t1r, mt, sy_out, sy_in, t2p, t2d, t2s, t2g,
     sp, sp_out, sp_in, sens,
-    ssem, rsem, asem, bsem, bfar, lsem, isem, gs, gh, gr, xs, xh, xr, vs, vh, vr, ds_, dr_, rs_, rr_, zr_,
+    ssem, rsem, asem, bsem, bfar, lsem, isem, gs, gh, gr, xs, xh, xr, vs, vh, vr, cs, ch, cr, ds_, dr_, rs_, rr_, zr_,
 ):
     r, z, k, c = where_am_i()
     y, x = k // s.nx, lax.rem(k, s.nx)
@@ -174,9 +181,13 @@
     mine = half == c
     kk = lax.rem(k, s.kh)
     every = range(CHUNKS)
-    g_ring = Ring(s, r, z, g_ref, ga, CHUNKS, gs, gh, gr)
-    x_ring = Ring(s, r, z, xa.at[z], xa, CHUNKS, xs, xh, xr)
-    v_ring = Ring(s, r, z, grid.at[b, a, z], grid.at[b, a], 2, vs, vh, vr)
+    cuts = even(x_ref.shape[0], CHUNKS)
+    early = 2 * s.hops - 3
+    g_ring = Ring(s, r, z, g_ref, ga, cuts, gs, gh, gr)
+    x_ring = Ring(s, r, z, xa.at[z], xa, cuts, xs, xh, xr)
+    v_ring = Ring(s, r, z, grid.at[b, a, z], grid.at[b, a], even(s.fbh, 2), vs, vh, vr)
+    early_cuts = [(0, (early + 1) // 2), ((early + 1) // 2, early // 2)]
+    c_ring = Ring(s, r, z, c128.at[c, z], c128.at[c], early_cuts, cs, ch, cr)
 
     welcome = greet(s, r, z)
     inputs = (v_hbm, v_ref), (g_hbm, g_ref), (x_hbm, x_ref), (e_hbm, e_ref), (w_hbm, w_ref)
@@ -285,7 +296,7 @@
         lax.fori_loop(1, s.nk, scatter, 0)
         part_in[k, slots] = part[k, slots]
 
-    def round_sum(hs, batch):
+    def round_sum(hs):
         for h in hs:
             arrive(part_in.at[pl.ds(0, s.nk - 1), pl.ds(0, len(round_of(h)))], rr_.at[h])
         lo = round_of(hs[0])[0][0]
@@ -293,6 +304,11 @@
         slots = pl.ds(lo, n)
         c128[c, z, slots] = jnp.sum(part_in[:, slots].astype(F32), axis=0).astype(BF16)
 
+        return slots
+
+    def round_lift(h, batch):
+        slots = round_sum([h])
+
         def lift(t, _):
             send(
                 c128.at[c, z, slots], c128.at[c, z, slots], ssem.at[9 + batch], zr_.at[batch],
@@ -301,7 +317,6 @@
             return 0
 
         lax.fori_loop(1, s.nz, lift, 0)
-        return slots
 
     assert s.nx == s.ny and s.nx in (2, 4)
     nzh = s.nz // 2
@@ -391,32 +406,38 @@
             product(blk)
         round_scatter(h)
         if h == s.hops - 1:
+            round_sum(range(0, h))
+            c_ring.begin([0, 1])
+            x_ring.begin(every[:2])
             b_forward()
             hand_out(b_left)
             if s.ny > 2:
                 hand_out(b_right)
         g_ring.step(h + 1, every)
-        if h == s.hops - 2:
-            x_ring.begin(every[:4])
 
     round_start(s.hops)
+    if s.hops > 2:
+        c_ring.step(1, [0, 1])
+    x_ring.begin([2])
     round_scatter(s.hops)
-    round_sum(range(0, s.hops - 1), 0)
-    round_sum([s.hops - 1], 1)
+    round_lift(s.hops - 1, 0)
+    if s.hops > 2:
+        c_ring.step(2, [0, 1])
+    x_ring.begin([3, 4])
     for h in (s.hops - 1, s.hops):
         for _, blk in round_of(h):
             product(blk)
-
-    round_sum([s.hops], 2)
+    round_lift(s.hops, 1)
+    if s.hops > 2:
+        c_ring.step(3, [0, 1])
     x_ring.begin(every)
     b_finish()
     if s.ny > 2:
         hand_out(b_far)
 
-    early = round_of(s.hops - 2)[-1][0] + 1
-    arrive(c128.at[c, pl.ds(0, s.nz - 1), pl.ds(0, early)], zr_.at[0])
-    arrive(c128.at[c, pl.ds(0, s.nz - 1), pl.ds(0, s.nz - 1 - early)], zr_.at[1])
-    arrive(c128.at[c, pl.ds(0, s.nz - 1), pl.ds(0, 1)], zr_.at[2])
+    c_ring.step(s.hops, [0, 1])
+    arrive(c128.at[c, pl.ds(0, s.nz - 1), pl.ds(0, 2)], zr_.at[0])
+    arrive(c128.at[c, pl.ds(0, s.nz - 1), pl.ds(0, 1)], zr_.at[1])
     send(c128.at[c], c128.at[c], ssem.at[12], rsem.at[7], mate, z)
     arrive(vv.at[:, c], lsem)
     arrive(vv.at[:, 1 - c], rsem.at[6])
@@ -533,14 +554,15 @@
         prod = prod.reshape(2, s.fb, s.fb)
         sp[two] = prod
         sp_out[two] = prod.astype(BF16)
-        send(sp_out.at[two], sp_in.at[two], ssem.at[16], rsem.at[12], mate, z)
+        send(sp_out.at[two], sp_in.at[two], ssem.at[16], bsem.at[0, q], mate, z)
         return 0
 
     lax.fori_loop(0, s.nz // 4, back, 0)
     x_ring.step(3, every[6:])
     lax.fori_loop(s.nz // 4, s.nz // 2, back, 0)
-    arrive(sp_in, rsem.at[12])
     for q in range(s.nz):
+        if q % 2 == 0:
+            arrive(sp_in.at[pl.ds(0, 2)], bsem.at[0, q // 2])
         sens[q] = (sp[q] + sp_in[q].astype(F32)).astype(BF16)
 
     far = x_ring.block(0, s.hops)
@@ -577,9 +599,9 @@
     arrive(grid.at[pl.ds(0, s.ny - 1)], ssem.at[5])
     arrive(vv.at[:, c], ssem.at[6])
     arrive(t1s, ssem.at[8])
-    arrive(c128.at[c, pl.ds(0, s.nz - 1), pl.ds(0, early)], ssem.at[9])
-    arrive(c128.at[c, pl.ds(0, s.nz - 1), pl.ds(0, s.nz - 1 - early)], ssem.at[10])
-    arrive(c128.at[c, pl.ds(0, s.nz - 1), pl.ds(0, 1)], ssem.at[11])
+    c_ring.drain()
+    arrive(c128.at[c, pl.ds(0, s.nz - 1), pl.ds(0, 2)], ssem.at[9])
+    arrive(c128.at[c, pl.ds(0, s.nz - 1), pl.ds(0, 1)], ssem.at[10])
     arrive(c128.at[c], ssem.at[12])
     arrive(t2p, ssem.at[14])
     arrive(part.at[pl.ds(0, s.nk - 1)], ssem.at[15])
@@ -641,7 +663,7 @@
             vmem((s.nz, s.fb, s.fb), BF16),
             vmem((s.nz, s.fb, s.fb), BF16),
             dma((17,)),
-            dma((13,)),
+            dma((12,)),
             dma((4,)),
             dma((2, 4)),
             dma((4,)),
@@ -656,11 +678,14 @@
             dma((2,)),
             dma((2,)),
             dma((s.hops, 2)),
+            dma((2,)),
+            dma((2,)),
+            dma((s.hops, 2)),
             dma((s.hops + 1,)),
             dma((s.hops + 1,)),
             dma((s.hops + 1,)),
             dma((s.hops + 1,)),
-            dma((3,)),
+            dma((2,)),
         ],
         compiler_params=pltpu.CompilerParams(
             collective_id=0, has_side_effects=True, vmem_limit_bytes=VMEM_CAP

time: 103 us -> 103 us (level)
  no operation moved by 1% of the time
where the time goes in v5:
time: 103 us
  Pallas kernels  102 us (99%)
    pallas_call x1, Pallas kernels, local(): pl.pallas_call(functools.partial(whole_kernel, s), name='whole', out_shap...  102 us

profile of v5, /device:TPU:1, one launch (start us, length us, event | category | flops | bytes accessed | tf_op | source)
XLA Modules:
  0.0 103.1 jit_solution(11962345048381306738)
XLA Ops:
  0.0 102.3 %whole.1 = bf16[1024,256]{1,0:T(8,128)(2,1)S(1)} custom-call(bf16[1024,256]{1,0:T(8,128)(2,1)} %x_hbm.1, bf16[1024,256]{1,0:T(8,128)(2,1)} %g_hbm.1, f32[64,256]{1,0:T(8,128)} %bitcast.4, f32[16,1,128]{2,1,0:T(1,128)} %bitcast.5, bf16[8,256,256]{2,1,0:T(8,128)(2,1)} %bitcast.3), custom_call_target="tpu_custom_call" | custom-call | flops 60000002048 | bytes 16000000 | tf_op jit(solution)/shard_map/whole/pallas_call | solution.py:622
  102.3 0.8 copy.7

commit v6 on v5

--- a/solution.py
+++ b/solution.py
@@ -431,6 +431,7 @@
     if s.hops > 2:
         c_ring.step(3, [0, 1])
     x_ring.begin(every)
+    x_ring.step(1, every[:3])
     b_finish()
     if s.ny > 2:
         hand_out(b_far)
@@ -534,7 +535,7 @@
         return 0
 
     lax.fori_loop(1, s.nk, spread, 0)
-    x_ring.step(3, every[:6])
+    x_ring.step(3, every)
 
     @pl.when(mine)
     def _():
@@ -558,7 +559,6 @@
         return 0
 
     lax.fori_loop(0, s.nz // 4, back, 0)
-    x_ring.step(3, every[6:])
     lax.fori_loop(s.nz // 4, s.nz // 2, back, 0)
     for q in range(s.nz):
         if q % 2 == 0:

time: 103 us -> 103 us (level)
  no operation moved by 1% of the time
where the time goes in v6:
time: 103 us
  Pallas kernels  102 us (99%)
    pallas_call x1, Pallas kernels, local(): pl.pallas_call(functools.partial(whole_kernel, s), name='whole', out_shap...  102 us

profile of v6, /device:TPU:1, one launch (start us, length us, event | category | flops | bytes accessed | tf_op | source)
XLA Modules:
  0.0 103.1 jit_solution(17361989290982617673)
XLA Ops:
  0.0 102.3 %whole.1 = bf16[1024,256]{1,0:T(8,128)(2,1)S(1)} custom-call(bf16[1024,256]{1,0:T(8,128)(2,1)} %x_hbm.1, bf16[1024,256]{1,0:T(8,128)(2,1)} %g_hbm.1, f32[64,256]{1,0:T(8,128)} %bitcast.4, f32[16,1,128]{2,1,0:T(1,128)} %bitcast.5, bf16[8,256,256]{2,1,0:T(8,128)(2,1)} %bitcast.3), custom_call_target="tpu_custom_call" | custom-call | flops 60000002048 | bytes 16000000 | tf_op jit(solution)/shard_map/whole/pallas_call | solution.py:622
  102.3 0.8 copy.7

commit v7 on v6

--- a/solution.py
+++ b/solution.py
@@ -529,12 +529,12 @@
     arrive(t2d, rsem.at[10])
     t2s[...] = (t2p[...] + t2d[...]).astype(BF16).reshape(t2s.shape)
 
-    def spread(t, _):
-        k2 = lax.rem(k + t, s.nk)
+    steps = [(dy, dx) for dy in range(s.ny) for dx in range(s.nx) if dy or dx]
+    steps.sort(key=lambda o: -min(o[0], s.ny - o[0]) - min(o[1], s.nx - o[1]))
+    for dy, dx in steps:
+        k2 = lax.rem(y + dy, s.ny) * s.nx + lax.rem(x + dx, s.nx)
         send(t2s.at[c], t2g.at[kk, c], ssem.at[15], rsem.at[11], 2 * k2 + half, z)
-        return 0
-
-    lax.fori_loop(1, s.nk, spread, 0)
+
     x_ring.step(3, every)
 
     @pl.when(mine)

time: 103 us -> 103 us (level)
  no operation moved by 1% of the time
where the time goes in v7:
time: 103 us
  Pallas kernels  102 us (99%)
    pallas_call x1, Pallas kernels, local(): pl.pallas_call(functools.partial(whole_kernel, s), name='whole', out_shap...  102 us

profile of v7, /device:TPU:1, one launch (start us, length us, event | category | flops | bytes accessed | tf_op | source)
XLA Modules:
  0.0 102.8 jit_solution(9741273576022038694)
XLA Ops:
  0.0 102.0 %whole.1 = bf16[1024,256]{1,0:T(8,128)(2,1)S(1)} custom-call(bf16[1024,256]{1,0:T(8,128)(2,1)} %x_hbm.1, bf16[1024,256]{1,0:T(8,128)(2,1)} %g_hbm.1, f32[64,256]{1,0:T(8,128)} %bitcast.4, f32[16,1,128]{2,1,0:T(1,128)} %bitcast.5, bf16[8,256,256]{2,1,0:T(8,128)(2,1)} %bitcast.3), custom_call_target="tpu_custom_call" | custom-call | flops 60000002048 | bytes 16000000 | tf_op jit(solution)/shard_map/whole/pallas_call | solution.py:622
  102.0 0.8 copy.7
